TPU v7x, 256 devices: a whole 4x4x8 slice. The times are simulated.
256 devices in a mesh: dp: 16 (over z_hi, y), outer: 16 (over z_lo, x, core).
Axes of the slice: x: 4, y: 4, z: 8 (z_hi: 4, z_lo: 2; z = z_hi * 2 + z_lo), core: 2. Of those that a mesh axis runs over, the one named last changes fastest.
Arguments:
- targets: bfloat16 [1024, 256], P(('dp', 'outer')), may hold values from -6 to 6
- behaviors: bfloat16 [1024, 1536, 256], P(('dp', 'outer')), may hold values from -256 to 256
- topk_index: int32 [1024, 1024], P(('dp', 'outer')), may hold values from 0 to 1535, as said below
- target_ids: int32 [1024], P(('dp', 'outer')), may hold values from 0 to 1073741823
- behavior_ids: int32 [1024, 1536], P(('dp', 'outer')), may hold values from 0 to 1073741823, as said below
- target_codes: int32 [1024], P(('dp', 'outer')), may hold values from 0 to 1073741823
- behavior_codes: int32 [1024, 1536], P(('dp', 'outer')), may hold values from 0 to 1073741823
- labels: int32 [1024], P(('dp', 'outer')), may hold values from -1 to 1, as said below
- attn_weights: float32 [4, 256, 256], replicated, may hold values from -2 to 2
- dense_weights: float32 [512, 1024], replicated, may hold values from -0.25 to 0.25
- head_weights: float32 [2, 1024], replicated, may hold values from -0.6 to 0.6
- moments: float32 [2, 788480], P(None, ('dp', 'outer')), may hold values from -0.0018 to 0.0018, as said below
Outputs:
- new_attention: float32 [4, 256, 256], replicated
- new_dense: float32 [512, 1024], replicated
- new_head: float32 [2, 1024], replicated
- new_moments: float32 [2, 788480], P(None, ('dp', 'outer'))
- loss: float32 [], replicated
Inputs may be any that keep to these rules, and one draw needn't show every extreme that they name: `topk_index`: indices into a user's 1536 behaviors, distinct within a user. `behavior_ids`: item ids; a behavior may carry its own user's target id. `labels`: -1 marks a user without a label; user 1024 - 1 always has one. `moments`: row 1 is positive.
All inputs are finite; a program needn't handle non-finite values.
Results may differ from a plain program's by a relative error of at most 0.012.
The roundings to bfloat16 on the way count: a program that leaves them out, or rounds other values in their place, can miss the bound.
Values sent between devices are 32-bit elements; how exact they have to be, the bound alone decides.
No kernel may reach another device: no remote copies, remote signals or barrier semaphores. Data moves between devices by JAX's collectives and lax.ppermute only.
A program may use at most 64 MiB of HBM per device.

v0:
```python
import jax
import jax.numpy as jnp
from jax import lax
from jax.sharding import Mesh
from jax.sharding import PartitionSpec as P

D = 256
HEADS = 8
DH = 32
DP_OUTER = ("dp_0", "dp_1", "outer_0", "outer_1", "outer_2")


sim_weight = 4.0
masked_score = -1000000000.0
learn_rate = 0.001
first_decay = 0.9
second_decay = 0.99
adam_eps = 1e-08
first_fix = 1.0 - 0.9**20
second_fix = 1.0 - 0.99**20


def in_order(tiles, dim):
    lengths = list(tiles.shape[1:])
    lengths[dim] *= tiles.shape[0]
    return jnp.moveaxis(tiles, 0, dim).reshape(lengths)


def gather_in_order(x, axes, turns):
    tiles = x
    for k in turns:
        tiles = lax.all_gather(tiles, axes[k])
    done = turns[::-1]
    back = [done.index(k) for k in range(len(axes))]
    tiles = tiles.transpose(*back, *range(len(axes), tiles.ndim))
    return tiles.reshape(-1, *x.shape)


def gather_axes(x, axes, turns, dim):
    return in_order(gather_in_order(x, axes, turns), dim)


def count_bits(value):
    value = value - jnp.bitwise_and(jnp.right_shift(value, 1), jnp.int32(1431655765))
    value = jnp.bitwise_and(value, jnp.int32(858993459)) + jnp.bitwise_and(
        jnp.right_shift(value, 2), jnp.int32(858993459)
    )
    value = jnp.bitwise_and(value + jnp.right_shift(value, 4), jnp.int32(252645135))
    value = value + jnp.right_shift(value, 8)
    value = value + jnp.right_shift(value, 16)
    return jnp.bitwise_and(value, jnp.int32(63))


def block_loss(weights, targets, picked, similarity, excluded, labels):
    attention, dense, head_rows = weights
    attention_half = attention.astype(jnp.bfloat16)
    dense_half = dense.astype(jnp.bfloat16)
    user_count = picked.shape[0]
    pick_count = picked.shape[1]
    queries = jnp.dot(targets, attention_half[0], preferred_element_type=jnp.float32).astype(
        jnp.bfloat16
    )
    flat_rows = picked.reshape(user_count * pick_count, D)
    key_rows = jnp.dot(flat_rows, attention_half[1], preferred_element_type=jnp.float32).astype(
        jnp.bfloat16
    )
    value_rows = jnp.dot(flat_rows, attention_half[2], preferred_element_type=jnp.float32).astype(
        jnp.bfloat16
    )
    key_rows = key_rows.reshape(user_count, pick_count, HEADS, DH)
    value_rows = value_rows.reshape(user_count, pick_count, HEADS, DH)
    head_queries = queries.reshape(user_count, HEADS, DH)
    scores = jnp.einsum(
        "uhd,ukhd->uhk", head_queries, key_rows, preferred_element_type=jnp.float32
    ) * DH ** (-0.5)
    scores = scores + similarity[:, None, :]
    scores = jnp.where(excluded[:, None, :], masked_score, scores)
    attend = jax.nn.softmax(scores, axis=-1).astype(jnp.bfloat16)
    attended = jnp.einsum("uhk,ukhd->uhd", attend, value_rows, preferred_element_type=jnp.float32)
    attended = attended.astype(jnp.bfloat16).reshape(user_count, D)
    mixed_out = jnp.dot(attended, attention_half[3], preferred_element_type=jnp.float32).astype(
        jnp.bfloat16
    )
    inputs = jnp.concatenate([targets, mixed_out], axis=1)
    pre_act = jnp.dot(inputs, dense_half, preferred_element_type=jnp.float32) + head_rows[0]
    hidden = jax.nn.gelu(pre_act, approximate=False).astype(jnp.bfloat16)
    logits = jnp.dot(hidden, head_rows[1].astype(jnp.bfloat16), preferred_element_type=jnp.float32)
    labeled = labels >= 0
    target_click = jnp.where(labeled, labels, 0).astype(jnp.float32)
    per_user = jax.nn.softplus(logits) - target_click * logits
    return jnp.sum(jnp.where(labeled, per_user, 0.0))


def per_device(
    targets,
    behaviors,
    topk_index,
    target_ids,
    behavior_ids,
    target_codes,
    behavior_codes,
    labels,
    attn_weights,
    dense_weights,
    head_weights,
    moments,
):
    picked = jnp.take_along_axis(behaviors, topk_index[:, :, None], axis=1)
    picked_ids = jnp.take_along_axis(behavior_ids, topk_index, axis=1)
    picked_codes = jnp.take_along_axis(behavior_codes, topk_index, axis=1)
    excluded = picked_ids == target_ids[:, None]
    agreement = 15 - count_bits(jnp.bitwise_xor(picked_codes, target_codes[:, None]))
    similarity = sim_weight * agreement.astype(jnp.float32) / 15.0
    local_count = jnp.sum((labels >= 0).astype(jnp.float32))
    weights = (attn_weights, dense_weights, head_weights)

    def objective(params):
        return block_loss(params, targets, picked, similarity, excluded, labels)

    local_sum, pullback = jax.vjp(objective, weights)
    gradients = pullback(jnp.ones_like(local_sum))[0]
    flat_grads = jnp.concatenate([portion.reshape(-1) for portion in gradients])
    statistics = jnp.stack([local_sum, local_count])
    share_size = moments.shape[1]
    share_start = lax.axis_index(DP_OUTER) * share_size
    summed, totals = lax.psum((flat_grads, statistics), DP_OUTER)
    own_grads = lax.dynamic_slice_in_dim(summed, share_start, share_size)
    loss = totals[0] / totals[1]
    own_grads = own_grads / totals[1]
    flat_weights = jnp.concatenate([portion.reshape(-1) for portion in weights])
    own_weights = lax.dynamic_slice_in_dim(flat_weights, share_start, share_size)
    new_first = first_decay * moments[0] + (1.0 - first_decay) * own_grads
    new_second = second_decay * moments[1] + (1.0 - second_decay) * own_grads * own_grads
    new_share = own_weights - learn_rate * (new_first / first_fix) / (
        jnp.sqrt(new_second / second_fix) + adam_eps
    )
    new_flat = gather_axes(
        new_share, (("dp_0", "dp_1", "outer_0", "outer_1"), "outer_2"), (0, 1), 0
    )
    attn_size = attn_weights.size
    dense_size = dense_weights.size
    new_attention = new_flat[:attn_size].reshape(attn_weights.shape)
    new_dense = new_flat[attn_size : attn_size + dense_size].reshape(dense_weights.shape)
    new_head = new_flat[attn_size + dense_size :].reshape(head_weights.shape)
    return (new_attention, new_dense, new_head, jnp.stack([new_first, new_second]), loss)


def solution(mesh):
    finer = Mesh(
        mesh.devices.reshape(4, 4, 2, 4, 2), ("dp_0", "dp_1", "outer_0", "outer_1", "outer_2")
    )
    placed = (
        P(DP_OUTER, None),
        P(DP_OUTER, None, None),
        P(DP_OUTER, None),
        P(DP_OUTER),
        P(DP_OUTER, None),
        P(DP_OUTER),
        P(DP_OUTER, None),
        P(DP_OUTER),
        P(),
        P(),
        P(),
        P(None, DP_OUTER),
    )
    return jax.shard_map(
        per_device,
        mesh=finer,
        in_specs=placed,
        out_specs=(P(), P(), P(), P(None, DP_OUTER), P()),
        check_vma=False,
    )
```

profile of v0, /device:TPU:1, one launch (start us, length us, event | category | flops | bytes accessed | tf_op | source)
XLA Modules:
  0.0 722.6 jit_solution(10875771153624214791)
XLA Ops:
  7.2 0.9 fusion.48
  8.1 35.0 %gather_fusion.1 = s32[4096]{0:T(1024)S(1)} fusion(s32[4,1536]{1,0:T(4,128)S(1)} %copy-done.2, s32[4096]{0:T(1024)S(1)} %bitcast.141), kind=kCustom, calls=%fused_computation.clone | custom fusion | bytes 65536 | tf_op jit(solution)/shard_map/jit(take_along_axis)/gather | solution.py:109
  43.2 41.2 %gather_fusion = bf16[4096,256]{1,0:T(8,128)(2,1)} fusion(bf16[4,1536,256]{2,1,0:T(8,128)(2,1)S(1)} %copy-done, s32[4096]{0:T(1024)S(1)} %bitcast.142), kind=kCustom, calls=%fused_computation.2 | custom fusion | bytes 4227072 | tf_op jit(solution)/shard_map/jit(take_along_axis)/gather | solution.py:108
  84.4 1.3 convert_element_type.102
  85.8 1.9 broadcast_select_fusion
  87.7 2.1 convolution_convert_fusion.1
  89.8 2.0 convolution_convert_fusion
  91.8 4.1 copy.18
  96.0 4.5 reshape.219
  100.5 0.1 convolution_convert_fusion.9
  100.7 35.0 %gather_fusion.2 = s32[4096]{0:T(1024)S(1)} fusion(s32[4,1536]{1,0:T(4,128)S(1)} %copy-done.3, s32[4096]{0:T(1024)S(1)} %bitcast.143), kind=kCustom, calls=%fused_computation.1.clone | custom fusion | bytes 65536 | tf_op jit(solution)/shard_map/jit(take_along_axis)/gather | solution.py:110
  135.7 4.1 copy.19
  139.9 4.5 reshape.220
  144.4 3.0 fusion.7
  147.4 0.3 fusion.68
  147.8 0.1 fusion.63
  147.9 1.3 fusion.3
  149.3 0.1 convolution_convert_fusion.8
  149.4 2.0 multiply_convert_fusion.3
  151.5 0.7 select_reduce_fusion
  152.3 0.4 fusion.15
  152.7 0.2 fusion.11
  153.0 0.1 convolution_convert_fusion.7
  153.4 1.8 convert_bitcast_fusion
  155.2 0.1 fusion.69
  155.3 0.1 copy.20
  155.5 0.8 multiply_convert_fusion.1
  156.3 0.9 copy.40
  157.2 0.8 fusion.12
  158.0 0.8 copy-done.9
  158.8 1.3 fusion.1
  160.0 0.2 fusion.21
  160.2 0.1 select_multiply_fusion
  160.4 0.1 copy.21
  160.5 0.8 multiply_convert_fusion
  161.4 0.9 copy.41
  162.2 0.8 fusion.13
  163.0 0.8 copy-done.7
  163.8 1.3 fusion.5
  165.2 0.2 fusion.14
  165.5 0.8 copy.42
  166.3 0.4 copy-done.10
  166.7 0.5 copy.43
  167.2 1.9 pad_maximum_fusion
  169.2 1.5 pad_maximum_fusion.5
  170.7 82.2 %psum.15 = f32[2]{0:T(128)S(1)} all-reduce(f32[2]{0:T(128)S(1)} %pad_maximum_fusion.5), channel_id=1, replica_groups=mesh['dp_0'=4,'dp_1'=4,'outer_0'=2,'outer_1'=4,'outer_2'=2] {'dp_0','dp_..., use_global_device_ids=true, to_apply=%region_7.9 | all-reduce | flops 2 | bytes 16 | tf_op jit(solution)/shard_map/psum | solution.py:126
  252.9 1.8 copy.37
  254.7 0.5 copy.36
  255.3 0.6 dynamic-slice
  256.5 0.6 fusion.67
  257.2 181.8 %all-reduce.10.cloned.1.call-done = f32[788480]{0:T(1024)} async-done(((f32[788480]{0:T(1024)}), f32[788480]{0:T(1024)}) %all-reduce.10.cloned.1.call-update) | async-done | bytes 3153936 | tf_op jit(solution)/shard_map/psum | solution.py:126
  439.1 1.6 subtract_dynamic-update-slice_fusion
  440.7 1.1 copy-done.11
  441.9 223.9 %all-reduce.12.cloned.1.call-done = f32[394240]{0:T(1024)} async-done(((f32[394240]{0:T(1024)}), f32[394240]{0:T(1024)}) %all-reduce.12.cloned.1.call-update) | async-done | bytes 1576976
  665.8 3.6 reshape.256
  670.8 0.6 pad_maximum_fusion.1
  671.5 18.4 %all-gather.4.cloned.1.call-done = f32[256,3080]{1,0:T(8,128)} async-done(((f32[128,3080]{1,0:T(8,128)}), f32[256,3080]{1,0:T(8,128)}) %all-gather.4.cloned.1.call-update) | async-done | bytes 3153936 | tf_op jit(solution)/shard_map/all_gather | solution.py:32
  689.8 4.5 copy.23
  694.3 6.2 slice.55
  700.5 5.1 reshape_reshape.3
  705.5 3.2 slice.71
  708.7 1.5 slice.72
  710.2 2.3 slice.70
  712.5 2.5 reshape.232
  (76 shorter events, 1.5 us)
Async XLA Ops:
  7.2 36.0 %copy-start = (bf16[4,1536,256]{2,1,0:T(8,128)(2,1)S(1)}, bf16[4,1536,256]{2,1,0:T(8,128)(2,1)}, u32[]{:S(2)}) copy-start(bf16[4,1536,256]{2,1,0:T(8,128)(2,1)} %param.15) | copy-start | bytes 9437188
  7.2 1.0 copy-start.2
  7.2 431.8 %all-reduce.10.cloned.1.call-start = ((), (), s32[]{:S(2)}) async-start(), calls=%async_computation | async-start | bytes 6307840 | tf_op jit(solution)/shard_map/psum | solution.py:126
  43.2 42.5 %copy-start.13 = (s32[4,1024]{1,0:T(4,128)S(1)}, s32[4,1024]{1,0:T(4,128)}, u32[]{:S(2)}) copy-start(s32[4,1024]{1,0:T(4,128)} %param.16) | copy-start | bytes 49156
  43.2 42.5 %copy-start.19 = (s32[4]{0:T(128)S(1)}, s32[4]{0:T(128)}, u32[]{:S(2)}) copy-start(s32[4]{0:T(128)} %param.17) | copy-start | bytes 52
  89.8 2.0 copy-start.14
  96.0 4.5 copy-start.16
  96.0 4.8 copy-start.3
  144.3 3.0 copy-start.18
  144.3 3.5 copy-start.8
  147.4 2.1 slice-start
  147.9 3.6 copy-start.15
  147.9 3.6 copy-start.20
  149.3 3.0 copy-start.4
  157.2 1.6 copy-start.9
  162.2 1.6 copy-start.7
  165.1 1.6 copy-start.10
  169.1 83.8 %copy-start.5 = (f32[512,1024]{1,0:T(8,128)S(1)}, f32[512,1024]{1,0:T(8,128)}, u32[]{:S(2)}) copy-start(f32[512,1024]{1,0:T(8,128)} %param.23) | copy-start | bytes 6291460
  169.1 496.7 %all-reduce.12.cloned.1.call-start = ((), (), s32[]{:S(2)}) async-start(), calls=%async_computation.2 | async-start | bytes 3153920
  252.9 1.8 copy-start.12
  252.9 2.4 copy-start.21
  254.7 2.4 copy-start.17
  254.7 184.4 %copy-start.6 = (f32[64,8,8,128]{3,1,2,0:T(8,128)S(1)}, f32[64,8,8,128]{3,1,2,0:T(8,128)}, u32[]{:S(2)}) copy-start(f32[64,8,8,128]{3,1,2,0:T(8,128)} %copy.37) | copy-start | bytes 6291460
  440.7 1.1 copy-start.11
  441.9 247.9 %all-gather.4.cloned.1.call-start = ((), (), s32[]{:S(2)}) async-start(), calls=%async_computation.1 | async-start | bytes 4915200 | tf_op jit(solution)/shard_map/all_gather | solution.py:32
  708.7 6.3 copy-start.1
Sparse Core Ops, SparseCore 0:
  169.3 269.6 all-reduce.9
  445.0 220.8 all-reduce.11
  669.6 20.1 all-gather.3
where the time goes:
time: 723 us
  waiting for transfers between devices  424 us (59%)
  local copies, waits for them, and re-layouts  168 us (23%)
  blocking collectives  82.2 us (11%)
  matrix products  18.4 us (3%)
  between operations  17.3 us (2%)
  other arithmetic  12.6 us (2%)
    unnamed x4, waiting for transfers between devices  224 us
    psum x1, waiting for transfers between devices, per_device(): summed, totals = lax.psum((flat_grads, statistics), DP_OUTER)  182 us
    psum x1, blocking collectives, per_device(): summed, totals = lax.psum((flat_grads, statistics), DP_OUTER)  82.2 us
    gather x1, local copies, waits for them, and re-layouts, per_device(): picked = jnp.take_along_axis(behaviors, topk_index[:, :, None], axis=1)  41.2 us
    gather x2, local copies, waits for them, and re-layouts, per_device(): picked_codes = jnp.take_along_axis(behavior_codes, topk_index, axis=1)  35 us
    gather x2, local copies, waits for them, and re-layouts, per_device(): picked_ids = jnp.take_along_axis(behavior_ids, topk_index, axis=1)  35 us
    all_gather x1, waiting for transfers between devices, gather_in_order(): tiles = lax.all_gather(tiles, axes[k])  18.4 us
  transfers between devices with their start and end apart: 3, of which 3 were waited for; matrix products, arithmetic and copies ran while one was open for 1% of the time, Pallas kernels for 0%

commit v1 on v0

v1 whole, which is shorter than its diff:
```python
import jax
import jax.numpy as jnp
from jax import lax
from jax.experimental import pallas as pl
from jax.experimental.pallas import tpu as pltpu
from jax.sharding import Mesh
from jax.sharding import PartitionSpec as P

D = 256
HEADS = 8
DH = 32
FF = 1024
K = 1024
HIST = 1536
U = 4
LANES = 128
ROWS = 6160
SHARE = 3080
BLOCK = 385
MAIN = 24
CHUNK = 200
AXES = ("zh", "y", "zl", "x", "c")
SIZES = dict(zh=4, y=4, zl=2, x=4, c=2)

sim_weight = 4.0
masked_score = -1000000000.0
unpicked_score = -3e38
learn_rate = 0.001
first_decay = 0.9
second_decay = 0.99
adam_eps = 1e-08
first_fix = 1.0 - 0.9**20
second_fix = 1.0 - 0.99**20

f32 = jnp.float32
bf16 = jnp.bfloat16


def iota(shape, dim):
    return lax.broadcasted_iota(jnp.int32, shape, dim)


def dot(a, b, contract):
    return lax.dot_general(a, b, ((contract[:1], contract[1:]), ((), ())), preferred_element_type=f32)


def halves(x):
    high = x.astype(bf16)
    return jnp.concatenate([high, (x - high.astype(f32)).astype(bf16)], axis=0)


def both(x):
    n = x.shape[0] // 2
    return x[:n] + x[n:]


def count_bits(value):
    value = value - ((value >> 1) & 1431655765)
    value = (value & 858993459) + ((value >> 2) & 858993459)
    value = (value + (value >> 4)) & 252645135
    value = value + (value >> 8)
    value = value + (value >> 16)
    return value & 63


def window_rows(zh, y, zl, x, c):
    return BLOCK * (4 * zh + y) + MAIN * (8 * zl + 2 * x + c)


def windows(half):
    for i in range(4):
        for j in range(4):
            x, y = (i, j) if half == 0 else (j, i)
            for z in range(8):
                base = CHUNK * (4 * i + j)
                place = (z // 2, y, z % 2, x, half)
                yield base + MAIN * z, base + 8 * MAIN + z, window_rows(*place), place


def column(ref):
    at = iota((U, 1), 0)
    out = jnp.full((U, 1), ref[0], ref.dtype)
    for u in range(1, U):
        out = jnp.where(at == u, ref[u], out)
    return out


def grad_body(
    target_ids,
    target_codes,
    labels,
    targets,
    topk_index,
    behavior_ids,
    behavior_codes,
    behaviors_hbm,
    attn_hbm,
    dense_hbm,
    head,
    keep,
    send,
    rows,
    attn,
    dense,
    behaviors,
    sems,
):
    copies = [pltpu.make_async_copy(attn_hbm.at[i], attn.at[i], sems.at[i]) for i in range(4)]
    copies += [pltpu.make_async_copy(behaviors_hbm.at[u], behaviors.at[u], sems.at[4 + u]) for u in range(U)]
    copies += [pltpu.make_async_copy(dense_hbm, dense, sems.at[8])]
    order = [0, 1, 4, 5, 6, 7, 2, 3, 8]
    for i in order:
        copies[i].start()

    picked = []
    for u in range(U):
        index = topk_index[u : u + 1, :]
        coarse = jnp.where(iota((16, K), 0) == (index >> 7), 1.0, 0.0).astype(bf16)
        fine = jnp.where(iota((LANES, K), 0) == (index & 127), 1.0, 0.0).astype(bf16)
        table = dot(coarse, fine, (1, 1))
        picked.append(
            jnp.concatenate(
                [jnp.broadcast_to(table[k : k + 1, :], (HEADS, LANES)) for k in range(HIST // LANES)], axis=1
            )
        )
    agreement = 15 - count_bits(behavior_codes[...] ^ column(target_codes))
    similarity = sim_weight * agreement.astype(f32) / 15.0
    excluded = jnp.where(behavior_ids[...] == column(target_ids), 1.0, 0.0)

    def per_head(x):
        return jnp.concatenate([jnp.broadcast_to(x[u : u + 1, :], (HEADS, x.shape[1])) for u in range(U)], axis=0)

    similarity = per_head(similarity)
    excluded = per_head(excluded) > 0.5
    picked = jnp.concatenate(picked, axis=0) > 0.5
    head_mask = (iota((U * HEADS, D), 1) // DH) == (iota((U * HEADS, D), 0) % HEADS)

    def spread(x):
        return jnp.where(head_mask, per_head(x), 0.0)

    def fold(x):
        kept = jnp.where(head_mask, x, 0.0)
        return jnp.concatenate(
            [jnp.sum(kept[HEADS * u : HEADS * (u + 1)], axis=0, keepdims=True) for u in range(U)], axis=0
        )

    def rows_by_user(x, contract):
        out = []
        for u in range(U):
            out.append(both(dot(halves(x[HEADS * u : HEADS * (u + 1)]), behaviors[u], contract)))
        return jnp.concatenate(out, axis=0)

    goals = targets[...]
    copies[0].wait()
    queries = dot(goals, attn[0].astype(bf16), (1, 0)).astype(bf16).astype(f32)
    query_blocks = spread(queries)
    copies[1].wait()
    w_key = attn[1].astype(bf16)
    query_fold = dot(query_blocks.astype(bf16), w_key, (1, 1))
    for u in range(U):
        copies[4 + u].wait()
    scores = rows_by_user(query_fold, (1, 1)) * DH ** (-0.5) + similarity
    scores = jnp.where(excluded, masked_score, scores)
    scores = jnp.where(picked, scores, unpicked_score)
    top = jnp.max(scores, axis=1, keepdims=True)
    weight = jnp.exp(scores - top)
    weight = weight / jnp.sum(weight, axis=1, keepdims=True)
    attend = weight.astype(bf16)
    mean_rows = jnp.concatenate(
        [dot(attend[HEADS * u : HEADS * (u + 1)], behaviors[u], (1, 0)) for u in range(U)], axis=0
    )
    copies[2].wait()
    w_value = attn[2].astype(bf16)
    attended = fold(both(dot(halves(mean_rows), w_value, (1, 0)))).astype(bf16)
    copies[3].wait()
    w_out = attn[3].astype(bf16)
    mixed = dot(attended, w_out, (1, 0)).astype(bf16)
    copies[8].wait()
    w_top = dense[:D].astype(bf16)
    w_low = dense[D:].astype(bf16)
    pre = dot(goals, w_top, (1, 0)) + dot(mixed, w_low, (1, 0)) + head[0:1, :]
    inner = 0.5 * (1.0 + lax.erf(pre * 0.5**0.5))
    hidden = (pre * inner).astype(bf16).astype(f32)
    head_vector = head[1:2, :].astype(bf16).astype(f32)
    logits = jnp.sum(hidden * head_vector, axis=1, keepdims=True)
    marks = column(labels)
    labeled = marks >= 0
    click = jnp.where(labeled, marks, 0).astype(f32)
    small = jnp.exp(-jnp.abs(logits))
    soft = jnp.maximum(logits, 0.0) + jnp.log1p(small)
    loss = jnp.sum(jnp.where(labeled, soft - click * logits, 0.0), axis=0, keepdims=True)
    count = jnp.sum(jnp.where(labeled, 1.0, 0.0), axis=0, keepdims=True)

    chance = jnp.where(logits >= 0, 1.0, small) / (1.0 + small)
    d_logits = jnp.where(labeled, chance - click, 0.0)
    d_hidden = (d_logits * head_vector).astype(bf16).astype(f32)
    d_pre = d_hidden * (inner + pre * jnp.exp(-0.5 * pre * pre) * (2.0 * jnp.pi) ** -0.5)
    d_pre_halves = halves(d_pre)
    d_mixed = both(dot(d_pre_halves, w_low, (1, 1))).astype(bf16)
    d_attended = dot(d_mixed, w_out, (1, 1)).astype(bf16)
    d_blocks = spread(d_attended.astype(f32))
    value_fold = dot(d_blocks.astype(bf16), w_value, (1, 1))
    d_attend = rows_by_user(value_fold, (1, 1)).astype(bf16).astype(f32)
    d_scores = weight * (d_attend - jnp.sum(weight * d_attend, axis=1, keepdims=True))
    d_scores = jnp.where(excluded, 0.0, d_scores)
    score_rows = rows_by_user(d_scores, (1, 0)) * DH ** (-0.5)
    d_queries = fold(both(dot(halves(score_rows), w_key, (1, 0)))).astype(bf16)

    def outer(a, b):
        return dot(a, b, (0, 0))

    def twice(x):
        return jnp.concatenate([x, x], axis=0)

    grads = [
        outer(goals, d_queries),
        outer(halves(score_rows), twice(query_blocks.astype(bf16))),
        outer(halves(mean_rows), twice(d_blocks.astype(bf16))),
        outer(attended, d_mixed),
    ]
    for i in range(4):
        for part in range(2):
            rows[pl.ds(512 * i + part, D, stride=2), :] = grads[i][:, LANES * part : LANES * (part + 1)]
    for source in range(2):
        grad = outer(twice((goals, mixed)[source]), d_pre_halves)
        for part in range(8):
            rows[pl.ds(2048 + 2048 * source + part, D, stride=8), :] = grad[:, LANES * part : LANES * (part + 1)]
    d_bias = jnp.sum(d_pre, axis=0, keepdims=True)
    d_vector = jnp.sum(d_logits * hidden, axis=0, keepdims=True)
    for source in range(2):
        grad = (d_bias, d_vector)[source]
        for part in range(8):
            at = 6144 + 8 * source + part
            rows[at : at + 1, :] = grad[:, LANES * part : LANES * (part + 1)]

    lane = iota((8, LANES), 1)
    first = (iota((8, LANES), 0) == 0) & (lane < 2)
    front = jnp.where(lane == 0, loss, count)
    lane = iota((1, LANES), 1)
    back = jnp.where(lane == LANES - 2, loss, count)

    def place(half, out):
        for main, tail, start, where in windows(half):
            for k in range(0, MAIN, 8):
                piece = rows[start + k : start + k + 8, :]
                if where[2] == 1 and k == 0:
                    piece = jnp.where(first, front, piece)
                out[main + k : main + k + 8, :] = piece
            last = rows[start + MAIN : start + MAIN + 1, :]
            if where[2] == 0:
                last = jnp.where(lane >= LANES - 2, back, last)
            out[tail : tail + 1, :] = last

    core = lax.axis_index("c")

    @pl.when(core == 0)
    def _():
        place(0, keep)
        place(1, send)

    @pl.when(core == 1)
    def _():
        place(1, keep)
        place(0, send)


VMEM = pl.BlockSpec(memory_space=pltpu.VMEM)
SMEM = pl.BlockSpec(memory_space=pltpu.SMEM)
ANY = pl.BlockSpec(memory_space=pl.ANY)
PARAMS = pltpu.CompilerParams(vmem_limit_bytes=50 * 2**20)


def vmem(*shape):
    return jax.ShapeDtypeStruct(shape, f32)


def call(body, outs, *args, specs=None, out_specs=None, scratch=()):
    return pl.pallas_call(
        body,
        out_shape=outs,
        in_specs=specs or [VMEM] * len(args),
        out_specs=out_specs or jax.tree.map(lambda _: VMEM, outs),
        scratch_shapes=scratch,
        compiler_params=PARAMS,
    )(*args)


def position(stage):
    x, y, c = (lax.axis_index(a) for a in ("x", "y", "c"))
    return jnp.where((c == 0) == (stage == 0), x, y)


def split_body(stage, parts):
    def body(*refs):
        sources, outs = refs[:parts], refs[parts:]
        size = outs[0].shape[0]
        at = position(stage)
        for k in range(4):
            start = pl.multiple_of(((at + k) % 4) * size, 8)
            total = sources[0][pl.ds(start, size), :]
            for s in sources[1:]:
                total = total + s[pl.ds(start, size), :]
            outs[k][...] = total

    return body


def z_split_body(*refs):
    sources, out = refs[:4], refs[4]
    total = sources[0][...] + sources[1][...] + sources[2][...] + sources[3][...]
    for z in range(8):
        out[z, :MAIN, :] = total[MAIN * z : MAIN * (z + 1)]
        tail = total[8 * MAIN + z : 8 * MAIN + z + 1]
        out[z, MAIN:, :] = jnp.where(iota((8, LANES), 0) == 0, tail, 0.0)


def adam_body(parts, moments, spread, new_moments, loss_out):
    total = parts[0]
    for z in range(1, 8):
        total = total + parts[z]
    zl, x, c = (lax.axis_index(a) for a in ("zl", "x", "c"))
    shift = 8 * (8 * zl + 2 * x + c)
    tail = total[MAIN : MAIN + 1]
    line = jnp.where(zl == 0, tail, total[0:1])
    lane = iota((1, LANES), 1)
    loss_at = jnp.where(zl == 0, LANES - 2, 0)
    loss = jnp.sum(jnp.where(lane == loss_at, line, 0.0), axis=1, keepdims=True)
    count = jnp.sum(jnp.where(lane == loss_at + 1, line, 0.0), axis=1, keepdims=True)
    loss_out[...] = loss / count
    lanes = iota((32, LANES), 1)
    turned = pltpu.roll(total, (LANES - shift) % LANES, 1)
    after = pltpu.roll(turned, 31, 0)
    grads = jnp.where(lanes < LANES - shift, turned, after) / count
    old = []
    for k in range(24):
        old.append(moments[:, LANES * k : LANES * (k + 1)])
    last = moments[:, SHARE - LANES :]
    last = jnp.where(iota((2, LANES), 1) < SHARE - 24 * LANES, pltpu.roll(last, SHARE - 24 * LANES, 1), 1.0)
    old.append(last)
    one = jnp.ones((7, LANES), f32)
    first = jnp.concatenate([o[0:1] for o in old] + [one], axis=0)
    second = jnp.concatenate([o[1:2] for o in old] + [one], axis=0)
    new_first = first_decay * first + (1.0 - first_decay) * grads
    new_second = second_decay * second + (1.0 - second_decay) * grads * grads
    for k in range(25):
        wide = min(LANES, SHARE - LANES * k)
        new_moments[0:1, LANES * k : LANES * k + wide] = new_first[k : k + 1, :wide]
        new_moments[1:2, LANES * k : LANES * k + wide] = new_second[k : k + 1, :wide]
    step = learn_rate * (new_first / first_fix) / (jnp.sqrt(new_second / second_fix) + adam_eps)
    flat = iota((32, LANES), 0) * LANES + lanes
    step = jnp.where(flat < SHARE, step, 0.0)
    turned = pltpu.roll(step, shift, 1)
    before = pltpu.roll(turned, 1, 0)
    step = jnp.where(lanes >= shift, turned, before)
    for z in range(8):
        spread[z] = step


def z_join_body(parts, out):
    for z in range(8):
        out[MAIN * z : MAIN * (z + 1), :] = parts[z, :MAIN, :]
        out[8 * MAIN + z : 8 * MAIN + z + 1, :] = parts[z, MAIN : MAIN + 1, :]


def join_body(stage):
    def body(*refs):
        sources, out = refs[:4], refs[4]
        size = sources[0].shape[0]
        at = position(stage)
        for k in range(4):
            start = pl.multiple_of(((at + 4 - k) % 4) * size, 8)
            out[pl.ds(start, size), :] = sources[k][...]

    return body


def apply_body(mine, other, attn, dense, head, new_attn, new_dense, new_head, rows):
    def place(half, source):
        for main, tail, start, where in windows(half):
            rows[start + 1 : start + MAIN, :] = source[main + 1 : main + MAIN, :]

    def joints(even, odd):
        firsts, lasts = {}, {}
        for half, source in ((0, even), (1, odd)):
            for main, tail, start, where in windows(half):
                firsts[start] = (source, main)
                lasts[start + MAIN] = (source, tail)
        for at in sorted(firsts | lasts):
            total = [r[m : m + 1, :] for r, m in (d[at] for d in (firsts, lasts) if at in d)]
            rows[at : at + 1, :] = sum(total[1:], total[0])

    core = lax.axis_index("c")
    for c in range(2):

        @pl.when(core == c)
        def _():
            place(c, mine)
            place(1 - c, other)
            joints(*((mine, other) if c == 0 else (other, mine)))

    for i in range(4):
        for part in range(2):
            lanes = slice(LANES * part, LANES * (part + 1))
            new_attn[i, :, lanes] = attn[i, :, lanes] - rows[pl.ds(512 * i + part, D, stride=2), :]
    for part in range(8):
        lanes = slice(LANES * part, LANES * (part + 1))
        new_dense[:, lanes] = dense[:, lanes] - rows[pl.ds(2048 + part, 2 * D, stride=8), :]
    for source in range(2):
        for part in range(8):
            lanes = slice(LANES * part, LANES * (part + 1))
            at = 6144 + 8 * source + part
            new_head[source : source + 1, lanes] = head[source : source + 1, lanes] - rows[at : at + 1, :]


def places():
    for zh in range(4):
        for y in range(4):
            for zl in range(2):
                for x in range(4):
                    for c in range(2):
                        yield zh, y, zl, x, c


def number(zh, y, zl, x, c):
    return (((zh * 4 + y) * 2 + zl) * 4 + x) * 2 + c


def turn(stage, k):
    pairs = []
    for zh, y, zl, x, c in places():
        along_x = (c == 0) == (stage == 0)
        goal = (zh, y, zl, (x + k) % 4, c) if along_x else (zh, (y + k) % 4, zl, x, c)
        pairs.append((number(zh, y, zl, x, c), number(*goal)))
    return pairs


def swap(x):
    return lax.ppermute(x, "c", [(0, 1), (1, 0)])


def gradient_windows(targets, behaviors, topk_index, target_ids, behavior_ids, target_codes, behavior_codes, labels, attn_weights, dense_weights, head_weights):
    return call(
        grad_body,
        (vmem(3200, LANES), vmem(3200, LANES)),
        target_ids,
        target_codes,
        labels,
        targets,
        topk_index,
        behavior_ids,
        behavior_codes,
        behaviors,
        attn_weights,
        dense_weights,
        head_weights,
        specs=[SMEM] * 3 + [VMEM] * 4 + [ANY] * 3 + [VMEM],
        scratch=[
            pltpu.VMEM((ROWS, LANES), f32),
            pltpu.VMEM((4, D, D), f32),
            pltpu.VMEM((2 * D, FF), f32),
            pltpu.VMEM((U, HIST, D), bf16),
            pltpu.SemaphoreType.DMA((9,)),
        ],
    )


def per_device(
    targets,
    behaviors,
    topk_index,
    target_ids,
    behavior_ids,
    target_codes,
    behavior_codes,
    labels,
    attn_weights,
    dense_weights,
    head_weights,
    moments,
):
    keep, send = gradient_windows(
        targets, behaviors, topk_index, target_ids, behavior_ids, target_codes, behavior_codes, labels, attn_weights, dense_weights, head_weights
    )
    own, *sent = call(split_body(0, 2), (vmem(800, LANES),) * 4, keep, swap(send))
    got = [lax.ppermute(s, AXES, turn(0, k + 1)) for k, s in enumerate(sent)]
    own, *sent = call(split_body(1, 4), (vmem(CHUNK, LANES),) * 4, own, *got)
    got = [lax.ppermute(s, AXES, turn(1, k + 1)) for k, s in enumerate(sent)]
    parts = call(z_split_body, vmem(8, 32, LANES), own, *got)
    parts = lax.all_to_all(parts, ("zh", "zl"), 0, 0, tiled=True)
    parts, new_moments, loss = call(
        adam_body, (vmem(8, 32, LANES), vmem(2, SHARE), vmem(1, 1)), parts, moments
    )
    parts = lax.all_to_all(parts, ("zh", "zl"), 0, 0, tiled=True)
    own = call(z_join_body, vmem(CHUNK, LANES), parts)
    got = [lax.ppermute(own, AXES, turn(1, k)) for k in range(1, 4)]
    own = call(join_body(1), vmem(800, LANES), own, *got)
    got = [lax.ppermute(own, AXES, turn(0, k)) for k in range(1, 4)]
    own = call(join_body(0), vmem(3200, LANES), own, *got)
    new_attention, new_dense, new_head = call(
        apply_body,
        (vmem(4, D, D), vmem(2 * D, FF), vmem(2, FF)),
        own,
        swap(own),
        attn_weights,
        dense_weights,
        head_weights,
        scratch=[pltpu.VMEM((ROWS, LANES), f32)],
    )
    return (new_attention, new_dense, new_head, new_moments, loss[0, 0])


def solution(mesh):
    finer = Mesh(mesh.devices.reshape(4, 4, 2, 4, 2), AXES)
    placed = (
        P(AXES, None),
        P(AXES, None, None),
        P(AXES, None),
        P(AXES),
        P(AXES, None),
        P(AXES),
        P(AXES, None),
        P(AXES),
        P(),
        P(),
        P(),
        P(None, AXES),
    )
    return jax.shard_map(
        per_device,
        mesh=finer,
        in_specs=placed,
        out_specs=(P(), P(), P(), P(None, AXES), P()),
        check_vma=False,
    )
```

time: 723 us -> 119 us (0.16)
  waiting for transfers between devices: 424 us -> 36.9 us
  local copies, waits for them, and re-layouts: 168 us -> 9.12 us
  blocking collectives: 82.2 us -> 25.3 us
  starting transfers between devices: 0.12 us -> 30.7 us
  matrix products: 18.4 us -> 0 us
  between operations: 17.3 us -> 0.74 us
  Pallas kernels: 0 us -> 16.2 us
  other arithmetic: 12.6 us -> 0 us
    unnamed x4 -> x0, waiting for transfers between devices: 224 us -> none
    psum x1 -> x0, waiting for transfers between devices: 182 us -> none  [per_device(): summed, totals = lax.psum((flat_grads, statistics), DP_OUTER)]
    gather x5 -> x0, local copies, waits for them, and re-layouts: 111 us -> none  [the longest x1 41.2 us: per_device(): picked = jnp.take_along_axis(behaviors, topk_index[:, :, None], axis=1)]
    psum x1 -> x0, blocking collectives: 82.2 us -> none  [per_device(): summed, totals = lax.psum((flat_grads, statistics), DP_OUTER)]
    ppermute x0 -> x14, waiting for transfers between devices: none -> 36.9 us  [the longest x3 11.7 us: per_device(): got = [lax.ppermute(own, AXES, turn(0, k)) for k in range(1, 4)]]
    ppermute x0 -> x14, starting transfers between devices: none -> 30.7 us  [the longest x2 17.2 us: swap(): return lax.ppermute(x, 'c', [(0, 1), (1, 0)])]
    all_to_all x0 -> x2, blocking collectives: none -> 25.3 us  [per_device(): parts = lax.all_to_all(parts, ('zh', 'zl'), 0, 0, tiled=True)]
    dot_general x18 -> x0, matrix products: 18.4 us -> none  [the longest x2 4.28 us: block_loss(): jnp.einsum('uhd,ukhd->uhk', head_queries, key_rows, preferred_element_typ...]
  transfers between devices with their start and end apart: 3 -> 14, of which waited for: 3 -> 11; matrix products, arithmetic and copies ran while one was open for 1% -> 0% of each run, Pallas kernels for 0% -> 0%
where the time goes in v1:
time: 119 us
  waiting for transfers between devices  36.9 us (31%)
  starting transfers between devices  30.7 us (26%)
  blocking collectives  25.3 us (21%)
  Pallas kernels  16.2 us (14%)
  local copies, waits for them, and re-layouts  9.12 us (8%)
    all_to_all x2, blocking collectives, per_device(): parts = lax.all_to_all(parts, ('zh', 'zl'), 0, 0, tiled=True)  25.3 us
    ppermute x2, starting transfers between devices, swap(): return lax.ppermute(x, 'c', [(0, 1), (1, 0)])  17.2 us
    pallas_call x9, Pallas kernels, call(): pl.pallas_call(body, out_shape=outs, in_specs=specs or [VMEM] * len(args)...  16.2 us
    ppermute x3, waiting for transfers between devices, per_device(): got = [lax.ppermute(own, AXES, turn(0, k)) for k in range(1, 4)]  11.7 us
    ppermute x3, waiting for transfers between devices, per_device(): got = [lax.ppermute(s, AXES, turn(0, k + 1)) for k, s in enumerate(sent)]  10 us
    unnamed x28, local copies, waits for them, and re-layouts  9.12 us
    ppermute x2, waiting for transfers between devices, swap(): return lax.ppermute(x, 'c', [(0, 1), (1, 0)])  6.47 us
    ppermute x3, waiting for transfers between devices, per_device(): got = [lax.ppermute(own, AXES, turn(1, k)) for k in range(1, 4)]  5.43 us
  transfers between devices with their start and end apart: 14, of which 11 were waited for; matrix products, arithmetic and copies ran while one was open for 0% of the time, Pallas kernels for 0%

profile of v1, /device:TPU:1, one launch (start us, length us, event | category | flops | bytes accessed | tf_op | source)
XLA Modules:
  0.0 118.9 jit_solution(9681607609350189660)
XLA Ops:
  0.6 0.0 copy-start
  0.6 1.2 %copy-done = f32[4,256,256]{2,1,0:T(8,128)S(1)} copy-done((f32[4,256,256]{2,1,0:T(8,128)S(1)}, f32[4,256,256]{2,1,0:T(8,128)}, u32[]{:S(2)}) %copy-start) | copy-done | bytes 1048600
  1.9 0.0 copy-start.2
  1.9 0.7 copy-done.2
  2.6 0.0 copy-start.5
  2.6 0.7 copy-done.5
  3.3 0.0 copy-start.6
  3.3 0.7 copy-done.6
  4.0 0.0 copy-start.7
  4.0 0.7 copy-done.7
  4.8 0.0 copy-start.8
  4.8 0.7 copy-done.8
  5.4 0.0 copy-start.9
  5.4 0.7 copy-done.9
  6.1 0.0 copy-start.10
  6.1 0.7 copy-done.10
  6.7 0.0 copy-start.11
  6.7 0.7 copy-done.11
  7.4 8.7 %shard_map.155 = (f32[3200,128]{1,0:T(8,128)S(1)}, f32[3200,128]{1,0:T(8,128)}) custom-call(s32[4]{0:T(128)S(1)} %copy-done.9, s32[4]{0:T(128)S(1)} %copy-done.10, s32[4]{0:T(128)S(1)} %copy-done.11, bf16[4,256]{1,0:T(4,128)(2,1)S(1)} %copy-done.8, s32[4,1024]{1,0:T(4,128)S(1)} %copy-done.7, s32[4,1536]{1,0:T(4,128)S(1)} %copy-done.5, ...), custom_call_target="tpu_custom_call" | custom-call | tf_op jit(solution)/shard_map/pallas_call | solution.py:278
  16.1 3.3 %collective-permute-start = (f32[3200,128]{1,0:T(8,128)}, f32[3200,128]{1,0:T(8,128)S(1)}, u32[]{:S(2)}, u32[]{:S(2)}) collective-permute-start(f32[3200,128]{1,0:T(8,128)} %get-tuple-element.22), channel_id=1, source_target_pairs={{0,1},{1,0},{2,3},{3,2},{4,5},{5,4},{6,7},{7,6},{8,9},{9,8},{10,11... | collective-permute-start | bytes 4915208 | tf_op jit(solution)/shard_map/ppermute | solution.py:438
  19.4 3.3 %collective-permute-done.refs_1_ = f32[3200,128]{1,0:T(8,128)S(1)} collective-permute-done((f32[3200,128]{1,0:T(8,128)}, f32[3200,128]{1,0:T(8,128)S(1)}, u32[]{:S(2)}, u32[]{:S(2)}) %collective-permute-start) | collective-permute-done | bytes 1638432 | tf_op jit(solution)/shard_map/ppermute | solution.py:438
  22.7 0.0 copy-start.12
  22.7 1.2 copy-done.12
  23.9 1.6 %shard_map.156 = (f32[800,128]{1,0:T(8,128)S(1)}, f32[800,128]{1,0:T(8,128)S(1)}, f32[800,128]{1,0:T(8,128)S(1)}, f32[800,128]{1,0:T(8,128)S(1)}) custom-call(f32[3200,128]{1,0:T(8,128)S(1)} %get-tuple-element.21.refs_0_, f32[3200,128]{1,0:T(8,128)} %copy-done.12), custom_call_target="tpu_custom_call" | custom-call | tf_op jit(solution)/shard_map/pallas_call | solution.py:278
  25.5 0.0 copy-start.4
  25.5 0.1 collective-permute-start.1
  25.6 2.2 %collective-permute-start.2 = (f32[800,128]{1,0:T(8,128)S(1)}, f32[800,128]{1,0:T(8,128)S(1)}, u32[]{:S(2)}, u32[]{:S(2)}) collective-permute-start(f32[800,128]{1,0:T(8,128)S(1)} %get-tuple-element.25), channel_id=1, source_target_pairs={{0,4},{1,33},{2,6},{3,35},{4,0},{5,37},{6,2},{7,39},{8,12},{9,41},... | collective-permute-start | bytes 1228808 | tf_op jit(solution)/shard_map/ppermute | solution.py:485
  27.8 1.1 collective-permute-start.3
  28.8 9.4 %collective-permute-done.1.refs_1_ = f32[800,128]{1,0:T(8,128)S(1)} collective-permute-done((f32[800,128]{1,0:T(8,128)S(1)}, f32[800,128]{1,0:T(8,128)S(1)}, u32[]{:S(2)}, u32[]{:S(2)}) %collective-permute-start.1) | collective-permute-done | bytes 409632 | tf_op jit(solution)/shard_map/ppermute | solution.py:485
  38.3 0.0 collective-permute-done.2.refs_2_
  38.3 0.6 collective-permute-done.3.refs_3_
  38.9 0.1 shard_map.157
  39.0 0.1 collective-permute-start.4
  39.1 2.3 %collective-permute-start.5 = (f32[200,128]{1,0:T(8,128)S(1)}, f32[200,128]{1,0:T(8,128)S(1)}, u32[]{:S(2)}, u32[]{:S(2)}) collective-permute-start(f32[200,128]{1,0:T(8,128)S(1)} %get-tuple-element.29), channel_id=1, source_target_pairs={{0,32},{1,5},{2,34},{3,7},{4,36},{5,1},{6,38},{7,3},{8,40},{9,13},... | collective-permute-start | bytes 307208 | tf_op jit(solution)/shard_map/ppermute | solution.py:487
  41.3 1.2 collective-permute-start.6
  42.5 2.7 %collective-permute-done.4.refs_1_ = f32[200,128]{1,0:T(8,128)S(1)} collective-permute-done((f32[200,128]{1,0:T(8,128)S(1)}, f32[200,128]{1,0:T(8,128)S(1)}, u32[]{:S(2)}, u32[]{:S(2)}) %collective-permute-start.4) | collective-permute-done | bytes 102432 | tf_op jit(solution)/shard_map/ppermute | solution.py:487
  45.2 0.0 collective-permute-done.5.refs_2_
  45.2 0.6 collective-permute-done.6.refs_3_
  45.8 15.0 %all_to_all.10.parts = f32[8,32,128]{2,1,0:T(8,128)S(1)} all-to-all(f32[8,32,128]{2,1,0:T(8,128)S(1)} %shard_map.158), channel_id=1, replica_groups=mesh['zh'=4,'y'=4,'zl'=2,'x'=4,'c'=2] {'zh','zl'}, dimensions={0} | all-to-all | bytes 262144 | tf_op jit(solution)/shard_map/all_to_all | solution.py:489
  60.8 0.0 copy-done.4
  60.8 0.8 shard_map.159
  61.6 10.3 %all_to_all.11.parts = f32[8,32,128]{2,1,0:T(8,128)S(1)} all-to-all(f32[8,32,128]{2,1,0:T(8,128)S(1)} %get-tuple-element.31), channel_id=1, replica_groups=mesh['zh'=4,'y'=4,'zl'=2,'x'=4,'c'=2] {'zh','zl'}, dimensions={0} | all-to-all | bytes 262144 | tf_op jit(solution)/shard_map/all_to_all | solution.py:493
  71.9 2.5 %collective-permute-start.9 = (f32[200,128]{1,0:T(8,128)S(1)}, f32[200,128]{1,0:T(8,128)S(1)}, u32[]{:S(2)}, u32[]{:S(2)}) collective-permute-start(f32[200,128]{1,0:T(8,128)S(1)} %shard_map.160.refs_0_), channel_id=1, source_target_pairs={{0,48},{1,7},{2,50},{3,1},{4,52},{5,3},{6,54},{7,5},{8,56},{9,15},... | collective-permute-start | bytes 307208 | tf_op jit(solution)/shard_map/ppermute | solution.py:495
  74.4 0.5 collective-permute-start.8
  74.9 0.2 collective-permute-start.7
  75.1 2.0 %collective-permute-done.9.refs_3_ = f32[200,128]{1,0:T(8,128)S(1)} collective-permute-done((f32[200,128]{1,0:T(8,128)S(1)}, f32[200,128]{1,0:T(8,128)S(1)}, u32[]{:S(2)}, u32[]{:S(2)}) %collective-permute-start.9) | collective-permute-done | bytes 102432 | tf_op jit(solution)/shard_map/ppermute | solution.py:495
  77.1 2.4 %collective-permute-done.8.refs_2_ = f32[200,128]{1,0:T(8,128)S(1)} collective-permute-done((f32[200,128]{1,0:T(8,128)S(1)}, f32[200,128]{1,0:T(8,128)S(1)}, u32[]{:S(2)}, u32[]{:S(2)}) %collective-permute-start.8) | collective-permute-done | bytes 102432 | tf_op jit(solution)/shard_map/ppermute | solution.py:495
  79.5 1.0 collective-permute-done.7.refs_1_
  80.6 0.0 copy-start.1
  80.6 0.0 copy-start.3
  80.6 2.2 %collective-permute-start.12 = (f32[800,128]{1,0:T(8,128)S(1)}, f32[800,128]{1,0:T(8,128)S(1)}, u32[]{:S(2)}, u32[]{:S(2)}) collective-permute-start(f32[800,128]{1,0:T(8,128)S(1)} %shard_map.161.refs_0_), channel_id=1, source_target_pairs={{0,6},{1,49},{2,0},{3,51},{4,2},{5,53},{6,4},{7,55},{8,14},{9,57},... | collective-permute-start | bytes 1228808 | tf_op jit(solution)/shard_map/ppermute | solution.py:497
  82.7 0.9 collective-permute-start.11
  83.6 0.4 collective-permute-start.10
  84.0 8.0 %collective-permute-done.12.refs_3_ = f32[800,128]{1,0:T(8,128)S(1)} collective-permute-done((f32[800,128]{1,0:T(8,128)S(1)}, f32[800,128]{1,0:T(8,128)S(1)}, u32[]{:S(2)}, u32[]{:S(2)}) %collective-permute-start.12) | collective-permute-done | bytes 409632 | tf_op jit(solution)/shard_map/ppermute | solution.py:497
  92.0 0.0 collective-permute-done.11.refs_2_
  92.0 3.7 %collective-permute-done.10.refs_1_ = f32[800,128]{1,0:T(8,128)S(1)} collective-permute-done((f32[800,128]{1,0:T(8,128)S(1)}, f32[800,128]{1,0:T(8,128)S(1)}, u32[]{:S(2)}, u32[]{:S(2)}) %collective-permute-start.10) | collective-permute-done | bytes 409632 | tf_op jit(solution)/shard_map/ppermute | solution.py:497
  95.7 0.1 shard_map.162.mine
  95.8 13.9 %collective-permute-start.13 = (f32[3200,128]{1,0:T(8,128)S(1)}, f32[3200,128]{1,0:T(8,128)S(1)}, u32[]{:S(2)}, u32[]{:S(2)}) collective-permute-start(f32[3200,128]{1,0:T(8,128)S(1)} %shard_map.162.mine), channel_id=1, source_target_pairs={{0,1},{1,0},{2,3},{3,2},{4,5},{5,4},{6,7},{7,6},{8,9},{9,8},{10,11... | collective-permute-start | bytes 4915208 | tf_op jit(solution)/shard_map/ppermute | solution.py:438
  109.8 3.1 %collective-permute-done.13.other = f32[3200,128]{1,0:T(8,128)S(1)} collective-permute-done((f32[3200,128]{1,0:T(8,128)S(1)}, f32[3200,128]{1,0:T(8,128)S(1)}, u32[]{:S(2)}, u32[]{:S(2)}) %collective-permute-start.13) | collective-permute-done | bytes 1638432 | tf_op jit(solution)/shard_map/ppermute | solution.py:438
  112.9 0.0 copy-start.13
  112.9 1.2 copy-done.13
  114.1 0.0 copy-done.1
  114.1 0.0 copy-done.3
  114.1 4.8 %shard_map.163 = (f32[4,256,256]{2,1,0:T(8,128)}, f32[512,1024]{1,0:T(8,128)}, f32[2,1024]{1,0:T(2,128)}) custom-call(f32[3200,128]{1,0:T(8,128)S(1)} %shard_map.162.mine, f32[3200,128]{1,0:T(8,128)} %copy-done.13, f32[4,256,256]{2,1,0:T(8,128)S(1)} %copy-done.1, f32[512,1024]{1,0:T(8,128)} %dense.1, f32[2,1024]{1,0:T(2,128)S(1)} %copy-done.3), custom_call_target="tpu_custom_call" | custom-call | tf_op jit(solution)/shard_map/pallas_call | solution.py:278
  (3 shorter events, 0.1 us)
Async XLA Ops:
  0.6 1.2 %copy-start = (f32[4,256,256]{2,1,0:T(8,128)S(1)}, f32[4,256,256]{2,1,0:T(8,128)}, u32[]{:S(2)}) copy-start(f32[4,256,256]{2,1,0:T(8,128)} %attn.1) | copy-start | bytes 3145732
  1.9 0.7 copy-start.2
  2.6 0.7 copy-start.5
  3.3 0.7 copy-start.6
  4.0 0.7 copy-start.7
  4.8 0.7 copy-start.8
  5.4 0.7 copy-start.9
  6.1 0.7 copy-start.10
  6.7 0.7 copy-start.11
  16.1 6.6 %collective-permute-start = (f32[3200,128]{1,0:T(8,128)}, f32[3200,128]{1,0:T(8,128)S(1)}, u32[]{:S(2)}, u32[]{:S(2)}) collective-permute-start(f32[3200,128]{1,0:T(8,128)} %get-tuple-element.22), channel_id=1, source_target_pairs={{0,1},{1,0},{2,3},{3,2},{4,5},{5,4},{6,7},{7,6},{8,9},{9,8},{10,11... | collective-permute-start | bytes 4915208 | tf_op jit(solution)/shard_map/ppermute | solution.py:438
  22.7 1.2 copy-start.12
  25.5 35.3 %copy-start.4 = (f32[2,3080]{1,0:T(2,128)S(1)}, f32[2,3080]{1,0:T(2,128)}, u32[]{:S(2)}) copy-start(f32[2,3080]{1,0:T(2,128)} %moments.1) | copy-start | bytes 73924
  25.5 12.8 %collective-permute-start.1 = (f32[800,128]{1,0:T(8,128)S(1)}, f32[800,128]{1,0:T(8,128)S(1)}, u32[]{:S(2)}, u32[]{:S(2)}) collective-permute-start(f32[800,128]{1,0:T(8,128)S(1)} %get-tuple-element.24), channel_id=1, source_target_pairs={{0,2},{1,17},{2,4},{3,19},{4,6},{5,21},{6,0},{7,23},{8,10},{9,25},... | collective-permute-start | bytes 1228808 | tf_op jit(solution)/shard_map/ppermute | solution.py:485
  25.6 12.7 %collective-permute-start.2 = (f32[800,128]{1,0:T(8,128)S(1)}, f32[800,128]{1,0:T(8,128)S(1)}, u32[]{:S(2)}, u32[]{:S(2)}) collective-permute-start(f32[800,128]{1,0:T(8,128)S(1)} %get-tuple-element.25), channel_id=1, source_target_pairs={{0,4},{1,33},{2,6},{3,35},{4,0},{5,37},{6,2},{7,39},{8,12},{9,41},... | collective-permute-start | bytes 1228808 | tf_op jit(solution)/shard_map/ppermute | solution.py:485
  27.8 11.1 %collective-permute-start.3 = (f32[800,128]{1,0:T(8,128)S(1)}, f32[800,128]{1,0:T(8,128)S(1)}, u32[]{:S(2)}, u32[]{:S(2)}) collective-permute-start(f32[800,128]{1,0:T(8,128)S(1)} %get-tuple-element.26), channel_id=1, source_target_pairs={{0,6},{1,49},{2,0},{3,51},{4,2},{5,53},{6,4},{7,55},{8,14},{9,57},... | collective-permute-start | bytes 1228808 | tf_op jit(solution)/shard_map/ppermute | solution.py:485
  39.0 6.2 %collective-permute-start.4 = (f32[200,128]{1,0:T(8,128)S(1)}, f32[200,128]{1,0:T(8,128)S(1)}, u32[]{:S(2)}, u32[]{:S(2)}) collective-permute-start(f32[200,128]{1,0:T(8,128)S(1)} %get-tuple-element.28), channel_id=1, source_target_pairs={{0,16},{1,3},{2,18},{3,5},{4,20},{5,7},{6,22},{7,1},{8,24},{9,11},... | collective-permute-start | bytes 307208 | tf_op jit(solution)/shard_map/ppermute | solution.py:487
  39.1 6.1 %collective-permute-start.5 = (f32[200,128]{1,0:T(8,128)S(1)}, f32[200,128]{1,0:T(8,128)S(1)}, u32[]{:S(2)}, u32[]{:S(2)}) collective-permute-start(f32[200,128]{1,0:T(8,128)S(1)} %get-tuple-element.29), channel_id=1, source_target_pairs={{0,32},{1,5},{2,34},{3,7},{4,36},{5,1},{6,38},{7,3},{8,40},{9,13},... | collective-permute-start | bytes 307208 | tf_op jit(solution)/shard_map/ppermute | solution.py:487
  41.3 4.4 %collective-permute-start.6 = (f32[200,128]{1,0:T(8,128)S(1)}, f32[200,128]{1,0:T(8,128)S(1)}, u32[]{:S(2)}, u32[]{:S(2)}) collective-permute-start(f32[200,128]{1,0:T(8,128)S(1)} %get-tuple-element.30), channel_id=1, source_target_pairs={{0,48},{1,7},{2,50},{3,1},{4,52},{5,3},{6,54},{7,5},{8,56},{9,15},... | collective-permute-start | bytes 307208 | tf_op jit(solution)/shard_map/ppermute | solution.py:487
  71.9 5.2 %collective-permute-start.9 = (f32[200,128]{1,0:T(8,128)S(1)}, f32[200,128]{1,0:T(8,128)S(1)}, u32[]{:S(2)}, u32[]{:S(2)}) collective-permute-start(f32[200,128]{1,0:T(8,128)S(1)} %shard_map.160.refs_0_), channel_id=1, source_target_pairs={{0,48},{1,7},{2,50},{3,1},{4,52},{5,3},{6,54},{7,5},{8,56},{9,15},... | collective-permute-start | bytes 307208 | tf_op jit(solution)/shard_map/ppermute | solution.py:495
  74.4 5.1 %collective-permute-start.8 = (f32[200,128]{1,0:T(8,128)S(1)}, f32[200,128]{1,0:T(8,128)S(1)}, u32[]{:S(2)}, u32[]{:S(2)}) collective-permute-start(f32[200,128]{1,0:T(8,128)S(1)} %shard_map.160.refs_0_), channel_id=1, source_target_pairs={{0,32},{1,5},{2,34},{3,7},{4,36},{5,1},{6,38},{7,3},{8,40},{9,13},... | collective-permute-start | bytes 307208 | tf_op jit(solution)/shard_map/ppermute | solution.py:495
  74.9 5.6 %collective-permute-start.7 = (f32[200,128]{1,0:T(8,128)S(1)}, f32[200,128]{1,0:T(8,128)S(1)}, u32[]{:S(2)}, u32[]{:S(2)}) collective-permute-start(f32[200,128]{1,0:T(8,128)S(1)} %shard_map.160.refs_0_), channel_id=1, source_target_pairs={{0,16},{1,3},{2,18},{3,5},{4,20},{5,7},{6,22},{7,1},{8,24},{9,11},... | collective-permute-start | bytes 307208 | tf_op jit(solution)/shard_map/ppermute | solution.py:495
  80.6 33.5 %copy-start.1 = (f32[4,256,256]{2,1,0:T(8,128)S(1)}, f32[4,256,256]{2,1,0:T(8,128)}, u32[]{:S(2)}) copy-start(f32[4,256,256]{2,1,0:T(8,128)} %attn.1) | copy-start | bytes 3145732
  80.6 33.5 %copy-start.3 = (f32[2,1024]{1,0:T(2,128)S(1)}, f32[2,1024]{1,0:T(2,128)}, u32[]{:S(2)}) copy-start(f32[2,1024]{1,0:T(2,128)} %head.3) | copy-start | bytes 24580
  80.6 11.4 %collective-permute-start.12 = (f32[800,128]{1,0:T(8,128)S(1)}, f32[800,128]{1,0:T(8,128)S(1)}, u32[]{:S(2)}, u32[]{:S(2)}) collective-permute-start(f32[800,128]{1,0:T(8,128)S(1)} %shard_map.161.refs_0_), channel_id=1, source_target_pairs={{0,6},{1,49},{2,0},{3,51},{4,2},{5,53},{6,4},{7,55},{8,14},{9,57},... | collective-permute-start | bytes 1228808 | tf_op jit(solution)/shard_map/ppermute | solution.py:497
  82.7 9.3 %collective-permute-start.11 = (f32[800,128]{1,0:T(8,128)S(1)}, f32[800,128]{1,0:T(8,128)S(1)}, u32[]{:S(2)}, u32[]{:S(2)}) collective-permute-start(f32[800,128]{1,0:T(8,128)S(1)} %shard_map.161.refs_0_), channel_id=1, source_target_pairs={{0,4},{1,33},{2,6},{3,35},{4,0},{5,37},{6,2},{7,39},{8,12},{9,41},... | collective-permute-start | bytes 1228808 | tf_op jit(solution)/shard_map/ppermute | solution.py:497
  83.6 12.1 %collective-permute-start.10 = (f32[800,128]{1,0:T(8,128)S(1)}, f32[800,128]{1,0:T(8,128)S(1)}, u32[]{:S(2)}, u32[]{:S(2)}) collective-permute-start(f32[800,128]{1,0:T(8,128)S(1)} %shard_map.161.refs_0_), channel_id=1, source_target_pairs={{0,2},{1,17},{2,4},{3,19},{4,6},{5,21},{6,0},{7,23},{8,10},{9,25},... | collective-permute-start | bytes 1228808 | tf_op jit(solution)/shard_map/ppermute | solution.py:497
  95.8 17.1 %collective-permute-start.13 = (f32[3200,128]{1,0:T(8,128)S(1)}, f32[3200,128]{1,0:T(8,128)S(1)}, u32[]{:S(2)}, u32[]{:S(2)}) collective-permute-start(f32[3200,128]{1,0:T(8,128)S(1)} %shard_map.162.mine), channel_id=1, source_target_pairs={{0,1},{1,0},{2,3},{3,2},{4,5},{5,4},{6,7},{7,6},{8,9},{9,8},{10,11... | collective-permute-start | bytes 4915208 | tf_op jit(solution)/shard_map/ppermute | solution.py:438
  112.9 1.2 %copy-start.13 = (f32[3200,128]{1,0:T(8,128)}, f32[3200,128]{1,0:T(8,128)S(1)}, u32[]{:S(2)}) copy-start(f32[3200,128]{1,0:T(8,128)S(1)} %collective-permute-done.13.other) | copy-start | bytes 4915204

commit v2 on v1

--- a/solution.py
+++ b/solution.py
@@ -18,7 +18,8 @@
 SHARE = 3080
 BLOCK = 385
 MAIN = 24
-CHUNK = 200
+UNIT = 104
+STREAM = 16 * UNIT
 AXES = ("zh", "y", "zl", "x", "c")
 SIZES = dict(zh=4, y=4, zl=2, x=4, c=2)
 
@@ -67,14 +68,33 @@
     return BLOCK * (4 * zh + y) + MAIN * (8 * zl + 2 * x + c)
 
 
+def along(stream, step):
+    return (stream + step) % 4
+
+
+def bit_of(bit, x, y):
+    v = x if bit < 2 else y
+    q = (v >> 1) & 1
+    return q if bit % 2 else (v & 1) ^ q
+
+
+def unbits(bits):
+    return bits[0] ^ (3 * bits[1]), bits[2] ^ (3 * bits[3])
+
+
 def windows(half):
-    for i in range(4):
-        for j in range(4):
-            x, y = (i, j) if half == 0 else (j, i)
-            for z in range(8):
-                base = CHUNK * (4 * i + j)
+    for part in range(2):
+        stream = 2 * half + part
+        for at in range(16):
+            bits = [0] * 4
+            for step in range(4):
+                bits[along(stream, step)] = (at >> (3 - step)) & 1
+            x, y = unbits(bits)
+            base = STREAM * part + UNIT * at
+            for k in range(4):
+                z = 4 * part + k
                 place = (z // 2, y, z % 2, x, half)
-                yield base + MAIN * z, base + 8 * MAIN + z, window_rows(*place), place
+                yield base + MAIN * k, base + 4 * MAIN + k, window_rows(*place), place
 
 
 def column(ref):
@@ -86,31 +106,23 @@
 
 
 def grad_body(
-    target_ids,
-    target_codes,
-    labels,
-    targets,
-    topk_index,
-    behavior_ids,
-    behavior_codes,
-    behaviors_hbm,
-    attn_hbm,
-    dense_hbm,
-    head,
-    keep,
-    send,
-    rows,
-    attn,
-    dense,
-    behaviors,
-    sems,
+    *refs,
 ):
+    sources, (keep, send, rows), targets_of, sems = refs[:11], refs[11:14], refs[14:25], refs[25]
+    target_ids, target_codes, labels, targets, topk_index, behavior_ids, behavior_codes, head, behaviors, attn, dense = targets_of
+    behaviors_hbm, attn_hbm, dense_hbm = sources[8:]
+    little = [pltpu.make_async_copy(a, b, sems.at[9 + i]) for i, (a, b) in enumerate(zip(sources[:8], targets_of[:8]))]
+    for i in (4, 0, 1, 2, 3, 5, 6, 7):
+        little[i].start()
     copies = [pltpu.make_async_copy(attn_hbm.at[i], attn.at[i], sems.at[i]) for i in range(4)]
     copies += [pltpu.make_async_copy(behaviors_hbm.at[u], behaviors.at[u], sems.at[4 + u]) for u in range(U)]
     copies += [pltpu.make_async_copy(dense_hbm, dense, sems.at[8])]
     order = [0, 1, 4, 5, 6, 7, 2, 3, 8]
     for i in order:
         copies[i].start()
+
+    for copy in little:
+        copy.wait()
 
     picked = []
     for u in range(U):
@@ -233,23 +245,15 @@
             at = 6144 + 8 * source + part
             rows[at : at + 1, :] = grad[:, LANES * part : LANES * (part + 1)]
 
-    lane = iota((8, LANES), 1)
-    first = (iota((8, LANES), 0) == 0) & (lane < 2)
-    front = jnp.where(lane == 0, loss, count)
-    lane = iota((1, LANES), 1)
-    back = jnp.where(lane == LANES - 2, loss, count)
+    lane = iota((UNIT - 4 * MAIN - 4, LANES), 1)
+    totals = jnp.where(lane == 0, loss, jnp.where(lane == 1, count, 0.0))
 
     def place(half, out):
-        for main, tail, start, where in windows(half):
-            for k in range(0, MAIN, 8):
-                piece = rows[start + k : start + k + 8, :]
-                if where[2] == 1 and k == 0:
-                    piece = jnp.where(first, front, piece)
-                out[main + k : main + k + 8, :] = piece
-            last = rows[start + MAIN : start + MAIN + 1, :]
-            if where[2] == 0:
-                last = jnp.where(lane >= LANES - 2, back, last)
-            out[tail : tail + 1, :] = last
+        for main, tail, start, _ in windows(half):
+            out[main : main + MAIN, :] = rows[start : start + MAIN, :]
+            out[tail : tail + 1, :] = rows[start + MAIN : start + MAIN + 1, :]
+        for unit in range(32):
+            out[UNIT * unit + 4 * MAIN + 4 : UNIT * (unit + 1), :] = totals
 
     core = lax.axis_index("c")
 
@@ -266,52 +270,66 @@
 
 VMEM = pl.BlockSpec(memory_space=pltpu.VMEM)
 SMEM = pl.BlockSpec(memory_space=pltpu.SMEM)
-ANY = pl.BlockSpec(memory_space=pl.ANY)
-PARAMS = pltpu.CompilerParams(vmem_limit_bytes=50 * 2**20)
+HBM = pl.BlockSpec(memory_space=pltpu.HBM)
 
 
 def vmem(*shape):
     return jax.ShapeDtypeStruct(shape, f32)
 
 
-def call(body, outs, *args, specs=None, out_specs=None, scratch=()):
+def call(body, outs, *args, specs=None, out_specs=None, scratch=(), limit=8):
     return pl.pallas_call(
         body,
         out_shape=outs,
         in_specs=specs or [VMEM] * len(args),
         out_specs=out_specs or jax.tree.map(lambda _: VMEM, outs),
         scratch_shapes=scratch,
-        compiler_params=PARAMS,
+        compiler_params=pltpu.CompilerParams(vmem_limit_bytes=limit * 2**20),
     )(*args)
 
 
-def position(stage):
+def bit_here(part, step):
     x, y, c = (lax.axis_index(a) for a in ("x", "y", "c"))
-    return jnp.where((c == 0) == (stage == 0), x, y)
-
-
-def split_body(stage, parts):
-    def body(*refs):
-        sources, outs = refs[:parts], refs[parts:]
-        size = outs[0].shape[0]
-        at = position(stage)
+    return jnp.where(
+        c == 0, bit_of_traced(along(part, step), x, y), bit_of_traced(along(2 + part, step), x, y)
+    )
+
+
+def bit_of_traced(bit, x, y):
+    v = x if bit < 2 else y
+    q = v // 2
+    return q if bit % 2 else (v + q) % 2
+
+
+def first_split_body(keep, got, *outs):
+    for part in range(2):
+        half = STREAM // 2
+        bit = bit_here(part, 0)
+        for k in range(2):
+            start = pl.multiple_of(STREAM * part + (bit if k == 0 else 1 - bit) * half, 8)
+            outs[2 * part + k][...] = keep[pl.ds(start, half), :] + got[pl.ds(start, half), :]
+
+
+def split_body(step):
+    def body(own_0, got_0, own_1, got_1, *outs):
+        for part, (own, got) in enumerate(((own_0, got_0), (own_1, got_1))):
+            half = own.shape[0] // 2
+            bit = bit_here(part, step)
+            for k in range(2):
+                start = pl.multiple_of((bit if k == 0 else 1 - bit) * half, 8)
+                outs[2 * part + k][...] = own[pl.ds(start, half), :] + got[pl.ds(start, half), :]
+
+    return body
+
+
+def z_split_body(own_0, got_0, own_1, got_1, out):
+    for part, (own, got) in enumerate(((own_0, got_0), (own_1, got_1))):
+        total = own[...] + got[...]
         for k in range(4):
-            start = pl.multiple_of(((at + k) % 4) * size, 8)
-            total = sources[0][pl.ds(start, size), :]
-            for s in sources[1:]:
-                total = total + s[pl.ds(start, size), :]
-            outs[k][...] = total
-
-    return body
-
-
-def z_split_body(*refs):
-    sources, out = refs[:4], refs[4]
-    total = sources[0][...] + sources[1][...] + sources[2][...] + sources[3][...]
-    for z in range(8):
-        out[z, :MAIN, :] = total[MAIN * z : MAIN * (z + 1)]
-        tail = total[8 * MAIN + z : 8 * MAIN + z + 1]
-        out[z, MAIN:, :] = jnp.where(iota((8, LANES), 0) == 0, tail, 0.0)
+            out[4 * part + k, :MAIN, :] = total[MAIN * k : MAIN * (k + 1)]
+            tail = total[4 * MAIN + k : 4 * MAIN + k + 1]
+            at = iota((8, LANES), 0)
+            out[4 * part + k, MAIN:, :] = jnp.where(at == 0, tail, jnp.where(at == 1, total[UNIT - 1 :], 0.0))
 
 
 def adam_body(parts, moments, spread, new_moments, loss_out):
@@ -320,12 +338,8 @@
         total = total + parts[z]
     zl, x, c = (lax.axis_index(a) for a in ("zl", "x", "c"))
     shift = 8 * (8 * zl + 2 * x + c)
-    tail = total[MAIN : MAIN + 1]
-    line = jnp.where(zl == 0, tail, total[0:1])
-    lane = iota((1, LANES), 1)
-    loss_at = jnp.where(zl == 0, LANES - 2, 0)
-    loss = jnp.sum(jnp.where(lane == loss_at, line, 0.0), axis=1, keepdims=True)
-    count = jnp.sum(jnp.where(lane == loss_at + 1, line, 0.0), axis=1, keepdims=True)
+    loss = total[MAIN + 1 : MAIN + 2, 0:1]
+    count = total[MAIN + 1 : MAIN + 2, 1:2]
     loss_out[...] = loss / count
     lanes = iota((32, LANES), 1)
     turned = pltpu.roll(total, (LANES - shift) % LANES, 1)
@@ -356,20 +370,23 @@
         spread[z] = step
 
 
-def z_join_body(parts, out):
-    for z in range(8):
-        out[MAIN * z : MAIN * (z + 1), :] = parts[z, :MAIN, :]
-        out[8 * MAIN + z : 8 * MAIN + z + 1, :] = parts[z, MAIN : MAIN + 1, :]
-
-
-def join_body(stage):
-    def body(*refs):
-        sources, out = refs[:4], refs[4]
-        size = sources[0].shape[0]
-        at = position(stage)
+def z_join_body(parts, *outs):
+    for part in range(2):
         for k in range(4):
-            start = pl.multiple_of(((at + 4 - k) % 4) * size, 8)
-            out[pl.ds(start, size), :] = sources[k][...]
+            outs[part][MAIN * k : MAIN * (k + 1), :] = parts[4 * part + k, :MAIN, :]
+            outs[part][4 * MAIN + k : 4 * MAIN + k + 1, :] = parts[4 * part + k, MAIN : MAIN + 1, :]
+        outs[part][4 * MAIN + 4 :, :] = jnp.zeros((UNIT - 4 * MAIN - 4, LANES), f32)
+
+
+def join_body(step):
+    def body(own_0, got_0, own_1, got_1, *outs):
+        for part, (own, got) in enumerate(((own_0, got_0), (own_1, got_1))):
+            half = own.shape[0]
+            bit = bit_here(part, step)
+            base, out = (STREAM * part, outs[0]) if step == 0 else (0, outs[part])
+            for k, source in enumerate((own, got)):
+                start = pl.multiple_of(base + (bit if k == 0 else 1 - bit) * half, 8)
+                out[pl.ds(start, half), :] = source[...]
 
     return body
 
@@ -425,13 +442,19 @@
     return (((zh * 4 + y) * 2 + zl) * 4 + x) * 2 + c
 
 
-def turn(stage, k):
+def flips(part, step):
     pairs = []
     for zh, y, zl, x, c in places():
-        along_x = (c == 0) == (stage == 0)
-        goal = (zh, y, zl, (x + k) % 4, c) if along_x else (zh, (y + k) % 4, zl, x, c)
-        pairs.append((number(zh, y, zl, x, c), number(*goal)))
+        bit = along(2 * c + part, step)
+        bits = [bit_of(b, x, y) for b in range(4)]
+        bits[bit] ^= 1
+        to_x, to_y = unbits(bits)
+        pairs.append((number(zh, y, zl, x, c), number(zh, to_y, zl, to_x, c)))
     return pairs
+
+
+def exchange(part, step, x):
+    return lax.ppermute(x, AXES, flips(part, step))
 
 
 def swap(x):
@@ -441,26 +464,40 @@
 def gradient_windows(targets, behaviors, topk_index, target_ids, behavior_ids, target_codes, behavior_codes, labels, attn_weights, dense_weights, head_weights):
     return call(
         grad_body,
-        (vmem(3200, LANES), vmem(3200, LANES)),
-        target_ids,
-        target_codes,
-        labels,
-        targets,
-        topk_index,
-        behavior_ids,
-        behavior_codes,
-        behaviors,
-        attn_weights,
-        dense_weights,
-        head_weights,
-        specs=[SMEM] * 3 + [VMEM] * 4 + [ANY] * 3 + [VMEM],
+        (vmem(2 * STREAM, LANES), vmem(2 * STREAM, LANES)),
+        *(
+            pltpu.with_memory_space_constraint(x, pltpu.HBM)
+            for x in (
+                target_ids,
+                target_codes,
+                labels,
+                targets,
+                topk_index,
+                behavior_ids,
+                behavior_codes,
+                head_weights,
+                behaviors,
+                attn_weights,
+                dense_weights,
+            )
+        ),
+        specs=[HBM] * 11,
         scratch=[
             pltpu.VMEM((ROWS, LANES), f32),
+            pltpu.SMEM((U,), jnp.int32),
+            pltpu.SMEM((U,), jnp.int32),
+            pltpu.SMEM((U,), jnp.int32),
+            pltpu.VMEM((U, D), bf16),
+            pltpu.VMEM((U, K), jnp.int32),
+            pltpu.VMEM((U, HIST), jnp.int32),
+            pltpu.VMEM((U, HIST), jnp.int32),
+            pltpu.VMEM((2, FF), f32),
+            pltpu.VMEM((U, HIST, D), bf16),
             pltpu.VMEM((4, D, D), f32),
             pltpu.VMEM((2 * D, FF), f32),
-            pltpu.VMEM((U, HIST, D), bf16),
-            pltpu.SemaphoreType.DMA((9,)),
+            pltpu.SemaphoreType.DMA((17,)),
         ],
+        limit=32,
     )
 
 
@@ -481,21 +518,30 @@
     keep, send = gradient_windows(
         targets, behaviors, topk_index, target_ids, behavior_ids, target_codes, behavior_codes, labels, attn_weights, dense_weights, head_weights
     )
-    own, *sent = call(split_body(0, 2), (vmem(800, LANES),) * 4, keep, swap(send))
-    got = [lax.ppermute(s, AXES, turn(0, k + 1)) for k, s in enumerate(sent)]
-    own, *sent = call(split_body(1, 4), (vmem(CHUNK, LANES),) * 4, own, *got)
-    got = [lax.ppermute(s, AXES, turn(1, k + 1)) for k, s in enumerate(sent)]
-    parts = call(z_split_body, vmem(8, 32, LANES), own, *got)
+    size = STREAM // 2
+    own_0, sent_0, own_1, sent_1 = call(first_split_body, (vmem(size, LANES),) * 4, keep, swap(send))
+    for step in range(4):
+        got_0, got_1 = exchange(0, step, sent_0), exchange(1, step, sent_1)
+        size //= 2
+        if step < 3:
+            own_0, sent_0, own_1, sent_1 = call(
+                split_body(step + 1), (vmem(size, LANES),) * 4, own_0, got_0, own_1, got_1
+            )
+    parts = call(z_split_body, vmem(8, 32, LANES), own_0, got_0, own_1, got_1)
     parts = lax.all_to_all(parts, ("zh", "zl"), 0, 0, tiled=True)
     parts, new_moments, loss = call(
         adam_body, (vmem(8, 32, LANES), vmem(2, SHARE), vmem(1, 1)), parts, moments
     )
     parts = lax.all_to_all(parts, ("zh", "zl"), 0, 0, tiled=True)
-    own = call(z_join_body, vmem(CHUNK, LANES), parts)
-    got = [lax.ppermute(own, AXES, turn(1, k)) for k in range(1, 4)]
-    own = call(join_body(1), vmem(800, LANES), own, *got)
-    got = [lax.ppermute(own, AXES, turn(0, k)) for k in range(1, 4)]
-    own = call(join_body(0), vmem(3200, LANES), own, *got)
+    size = UNIT
+    own_0, own_1 = call(z_join_body, (vmem(size, LANES),) * 2, parts)
+    for step in range(3, -1, -1):
+        got_0, got_1 = exchange(0, step, own_0), exchange(1, step, own_1)
+        size *= 2
+        outs = (vmem(size, LANES),) * 2 if step else (vmem(2 * size, LANES),)
+        own_0, *own_1 = call(join_body(step), outs, own_0, got_0, own_1, got_1)
+        own_1 = own_1[0] if step else None
+    own = own_0
     new_attention, new_dense, new_head = call(
         apply_body,
         (vmem(4, D, D), vmem(2 * D, FF), vmem(2, FF)),
@@ -505,6 +551,7 @@
         dense_weights,
         head_weights,
         scratch=[pltpu.VMEM((ROWS, LANES), f32)],
+        limit=20,
     )
     return (new_attention, new_dense, new_head, new_moments, loss[0, 0])
 

time: 119 us -> 111 us (0.933)
  local copies, waits for them, and re-layouts: 9.12 us -> 0.02 us
  waiting for transfers between devices: 36.9 us -> 41.5 us
  Pallas kernels: 16.2 us -> 11.6 us
    unnamed x28 -> x8, local copies, waits for them, and re-layouts: 9.12 us -> 0.02 us
    ppermute x12 -> x16, waiting for transfers between devices: 30.4 us -> 35.1 us  [exchange(): return lax.ppermute(x, AXES, flips(part, step))]
    pallas_call x9 -> x13, Pallas kernels: 16.2 us -> 11.6 us  [call(): pl.pallas_call(body, out_shape=outs, in_specs=specs or [VMEM] * len(args)...]
    ppermute x12 -> x16, starting transfers between devices: 13.5 us -> 14.8 us  [exchange(): return lax.ppermute(x, AXES, flips(part, step))]
  transfers between devices with their start and end apart: 14 -> 18, of which waited for: 11 -> 16; matrix products, arithmetic and copies ran while one was open for 0% -> 0% of each run, Pallas kernels for 0% -> 0%
where the time goes in v2:
time: 111 us
  waiting for transfers between devices  41.5 us (37%)
  starting transfers between devices  31 us (28%)
  blocking collectives  26.1 us (24%)
  Pallas kernels  11.6 us (10%)
    ppermute x16, waiting for transfers between devices, exchange(): return lax.ppermute(x, AXES, flips(part, step))  35.1 us
    all_to_all x2, blocking collectives, per_device(): parts = lax.all_to_all(parts, ('zh', 'zl'), 0, 0, tiled=True)  26.1 us
    ppermute x2, starting transfers between devices, swap(): return lax.ppermute(x, 'c', [(0, 1), (1, 0)])  16.2 us
    ppermute x16, starting transfers between devices, exchange(): return lax.ppermute(x, AXES, flips(part, step))  14.8 us
    pallas_call x13, Pallas kernels, call(): pl.pallas_call(body, out_shape=outs, in_specs=specs or [VMEM] * len(args)...  11.6 us
    ppermute x2, waiting for transfers between devices, swap(): return lax.ppermute(x, 'c', [(0, 1), (1, 0)])  6.45 us
  transfers between devices with their start and end apart: 18, of which 16 were waited for; matrix products, arithmetic and copies ran while one was open for 0% of the time, Pallas kernels for 0%

profile of v2, /device:TPU:1, one launch (start us, length us, event | category | flops | bytes accessed | tf_op | source)
XLA Modules:
  0.0 111.0 jit_solution(5552470227177234554)
XLA Ops:
  0.6 7.3 %shard_map.155 = (f32[3328,128]{1,0:T(8,128)S(1)}, f32[3328,128]{1,0:T(8,128)S(1)}) custom-call(s32[4]{0:T(128)} %refs_0_.1, s32[4]{0:T(128)} %refs_1_.1, s32[4]{0:T(128)} %refs_2_.1, bf16[4,256]{1,0:T(4,128)(2,1)} %refs_3_.1, s32[4,1024]{1,0:T(4,128)} %refs_4_.1, s32[4,1536]{1,0:T(4,128)} %refs_5_.1, s32[4,1536]{1,0:T(4,128)} %refs_6_.1, f32[2,1024]{1,0:T(2,128)} %head.1, ...), custom_call_target="tpu_custom_call" | custom-call | tf_op jit(solution)/shard_map/pallas_call | solution.py:281
  7.9 3.3 %collective-permute-start = (f32[3328,128]{1,0:T(8,128)S(1)}, f32[3328,128]{1,0:T(8,128)S(1)}, u32[]{:S(2)}, u32[]{:S(2)}) collective-permute-start(f32[3328,128]{1,0:T(8,128)S(1)} %get-tuple-element.38), channel_id=1, source_target_pairs={{0,1},{1,0},{2,3},{3,2},{4,5},{5,4},{6,7},{7,6},{8,9},{9,8},{10,11... | collective-permute-start | bytes 5111816 | tf_op jit(solution)/shard_map/ppermute | solution.py:461
  11.2 3.2 %collective-permute-done.got = f32[3328,128]{1,0:T(8,128)S(1)} collective-permute-done((f32[3328,128]{1,0:T(8,128)S(1)}, f32[3328,128]{1,0:T(8,128)S(1)}, u32[]{:S(2)}, u32[]{:S(2)}) %collective-permute-start) | collective-permute-done | bytes 1703968 | tf_op jit(solution)/shard_map/ppermute | solution.py:461
  14.4 0.2 shard_map.156
  14.6 0.1 collective-permute-start.1
  14.7 1.5 %collective-permute-start.2 = (f32[832,128]{1,0:T(8,128)S(1)}, f32[832,128]{1,0:T(8,128)S(1)}, u32[]{:S(2)}, u32[]{:S(2)}) collective-permute-start(f32[832,128]{1,0:T(8,128)S(1)} %get-tuple-element.42), channel_id=1, source_target_pairs={{0,6},{1,49},{2,4},{3,51},{4,2},{5,53},{6,0},{7,55},{8,14},{9,57},... | collective-permute-start | bytes 1277960 | tf_op jit(solution)/shard_map/ppermute | solution.py:457
  16.2 5.8 %collective-permute-done.1.got_0 = f32[832,128]{1,0:T(8,128)S(1)} collective-permute-done((f32[832,128]{1,0:T(8,128)S(1)}, f32[832,128]{1,0:T(8,128)S(1)}, u32[]{:S(2)}, u32[]{:S(2)}) %collective-permute-start.1) | collective-permute-done | bytes 426016 | tf_op jit(solution)/shard_map/ppermute | solution.py:457
  21.9 1.3 %collective-permute-done.2.got_1 = f32[832,128]{1,0:T(8,128)S(1)} collective-permute-done((f32[832,128]{1,0:T(8,128)S(1)}, f32[832,128]{1,0:T(8,128)S(1)}, u32[]{:S(2)}, u32[]{:S(2)}) %collective-permute-start.2) | collective-permute-done | bytes 426016 | tf_op jit(solution)/shard_map/ppermute | solution.py:457
  23.2 0.0 copy-start.3
  23.2 0.1 shard_map.157
  23.3 1.5 %collective-permute-start.3 = (f32[416,128]{1,0:T(8,128)S(1)}, f32[416,128]{1,0:T(8,128)S(1)}, u32[]{:S(2)}, u32[]{:S(2)}) collective-permute-start(f32[416,128]{1,0:T(8,128)S(1)} %get-tuple-element.44), channel_id=1, source_target_pairs={{0,6},{1,49},{2,4},{3,51},{4,2},{5,53},{6,0},{7,55},{8,14},{9,57},... | collective-permute-start | bytes 638984 | tf_op jit(solution)/shard_map/ppermute | solution.py:457
  24.8 0.9 collective-permute-start.4
  25.7 3.9 %collective-permute-done.3.got_0 = f32[416,128]{1,0:T(8,128)S(1)} collective-permute-done((f32[416,128]{1,0:T(8,128)S(1)}, f32[416,128]{1,0:T(8,128)S(1)}, u32[]{:S(2)}, u32[]{:S(2)}) %collective-permute-start.3) | collective-permute-done | bytes 213024 | tf_op jit(solution)/shard_map/ppermute | solution.py:457
  29.6 0.2 collective-permute-done.4.got_1
  29.9 1.0 collective-permute-start.5
  30.9 1.8 %collective-permute-start.6 = (f32[208,128]{1,0:T(8,128)S(1)}, f32[208,128]{1,0:T(8,128)S(1)}, u32[]{:S(2)}, u32[]{:S(2)}) collective-permute-start(f32[208,128]{1,0:T(8,128)S(1)} %get-tuple-element.50), channel_id=1, source_target_pairs={{0,48},{1,7},{2,50},{3,5},{4,52},{5,3},{6,54},{7,1},{8,56},{9,15},... | collective-permute-start | bytes 319496 | tf_op jit(solution)/shard_map/ppermute | solution.py:457
  32.7 0.8 collective-permute-done.5.got_0
  33.5 2.1 %collective-permute-done.6.got_1 = f32[208,128]{1,0:T(8,128)S(1)} collective-permute-done((f32[208,128]{1,0:T(8,128)S(1)}, f32[208,128]{1,0:T(8,128)S(1)}, u32[]{:S(2)}, u32[]{:S(2)}) %collective-permute-start.6) | collective-permute-done | bytes 106528 | tf_op jit(solution)/shard_map/ppermute | solution.py:457
  35.7 1.9 %collective-permute-start.7 = (f32[104,128]{1,0:T(8,128)S(1)}, f32[104,128]{1,0:T(8,128)S(1)}, u32[]{:S(2)}, u32[]{:S(2)}) collective-permute-start(f32[104,128]{1,0:T(8,128)S(1)} %get-tuple-element.52), channel_id=1, source_target_pairs={{0,48},{1,7},{2,50},{3,5},{4,52},{5,3},{6,54},{7,1},{8,56},{9,15},... | collective-permute-start | bytes 159752 | tf_op jit(solution)/shard_map/ppermute | solution.py:457
  37.6 0.0 collective-permute-start.8
  37.6 2.4 %collective-permute-done.7.got_0 = f32[104,128]{1,0:T(8,128)S(1)} collective-permute-done((f32[104,128]{1,0:T(8,128)S(1)}, f32[104,128]{1,0:T(8,128)S(1)}, u32[]{:S(2)}, u32[]{:S(2)}) %collective-permute-start.7) | collective-permute-done | bytes 53280 | tf_op jit(solution)/shard_map/ppermute | solution.py:457
  39.9 0.6 collective-permute-done.8.got_1
  40.6 15.8 %all_to_all.10.parts = f32[8,32,128]{2,1,0:T(8,128)S(1)} all-to-all(f32[8,32,128]{2,1,0:T(8,128)S(1)} %shard_map.160), channel_id=1, replica_groups=mesh['zh'=4,'y'=4,'zl'=2,'x'=4,'c'=2] {'zh','zl'}, dimensions={0} | all-to-all | bytes 262144 | tf_op jit(solution)/shard_map/all_to_all | solution.py:531
  56.3 0.0 copy-done.3
  56.3 0.8 shard_map.161
  57.1 10.3 %all_to_all.11.parts = f32[8,32,128]{2,1,0:T(8,128)S(1)} all-to-all(f32[8,32,128]{2,1,0:T(8,128)S(1)} %get-tuple-element.55), channel_id=1, replica_groups=mesh['zh'=4,'y'=4,'zl'=2,'x'=4,'c'=2] {'zh','zl'}, dimensions={0} | all-to-all | bytes 262144 | tf_op jit(solution)/shard_map/all_to_all | solution.py:535
  67.4 1.3 %collective-permute-start.9 = (f32[104,128]{1,0:T(8,128)S(1)}, f32[104,128]{1,0:T(8,128)S(1)}, u32[]{:S(2)}, u32[]{:S(2)}) collective-permute-start(f32[104,128]{1,0:T(8,128)S(1)} %get-tuple-element.56.own_0), channel_id=1, source_target_pairs={{0,48},{1,7},{2,50},{3,5},{4,52},{5,3},{6,54},{7,1},{8,56},{9,15},... | collective-permute-start | bytes 159752 | tf_op jit(solution)/shard_map/ppermute | solution.py:457
  68.7 0.0 collective-permute-start.10
  68.7 3.3 %collective-permute-done.9.got_0 = f32[104,128]{1,0:T(8,128)S(1)} collective-permute-done((f32[104,128]{1,0:T(8,128)S(1)}, f32[104,128]{1,0:T(8,128)S(1)}, u32[]{:S(2)}, u32[]{:S(2)}) %collective-permute-start.9) | collective-permute-done | bytes 53280 | tf_op jit(solution)/shard_map/ppermute | solution.py:457
  72.0 0.0 collective-permute-done.10.got_1
  72.0 0.1 collective-permute-start.11
  72.1 1.7 %collective-permute-start.12 = (f32[208,128]{1,0:T(8,128)S(1)}, f32[208,128]{1,0:T(8,128)S(1)}, u32[]{:S(2)}, u32[]{:S(2)}) collective-permute-start(f32[208,128]{1,0:T(8,128)S(1)} %get-tuple-element.59.own_1), channel_id=1, source_target_pairs={{0,48},{1,7},{2,50},{3,5},{4,52},{5,3},{6,54},{7,1},{8,56},{9,15},... | collective-permute-start | bytes 319496 | tf_op jit(solution)/shard_map/ppermute | solution.py:457
  73.9 1.8 %collective-permute-done.11.got_0 = f32[208,128]{1,0:T(8,128)S(1)} collective-permute-done((f32[208,128]{1,0:T(8,128)S(1)}, f32[208,128]{1,0:T(8,128)S(1)}, u32[]{:S(2)}, u32[]{:S(2)}) %collective-permute-start.11) | collective-permute-done | bytes 106528 | tf_op jit(solution)/shard_map/ppermute | solution.py:457
  75.7 1.5 %collective-permute-done.12.got_1 = f32[208,128]{1,0:T(8,128)S(1)} collective-permute-done((f32[208,128]{1,0:T(8,128)S(1)}, f32[208,128]{1,0:T(8,128)S(1)}, u32[]{:S(2)}, u32[]{:S(2)}) %collective-permute-start.12) | collective-permute-done | bytes 106528 | tf_op jit(solution)/shard_map/ppermute | solution.py:457
  77.2 1.3 %collective-permute-start.13 = (f32[416,128]{1,0:T(8,128)S(1)}, f32[416,128]{1,0:T(8,128)S(1)}, u32[]{:S(2)}, u32[]{:S(2)}) collective-permute-start(f32[416,128]{1,0:T(8,128)S(1)} %get-tuple-element.60.own_0), channel_id=1, source_target_pairs={{0,6},{1,49},{2,4},{3,51},{4,2},{5,53},{6,0},{7,55},{8,14},{9,57},... | collective-permute-start | bytes 638984 | tf_op jit(solution)/shard_map/ppermute | solution.py:457
  78.5 0.0 collective-permute-start.14
  78.5 4.7 %collective-permute-done.13.got_0 = f32[416,128]{1,0:T(8,128)S(1)} collective-permute-done((f32[416,128]{1,0:T(8,128)S(1)}, f32[416,128]{1,0:T(8,128)S(1)}, u32[]{:S(2)}, u32[]{:S(2)}) %collective-permute-start.13) | collective-permute-done | bytes 213024 | tf_op jit(solution)/shard_map/ppermute | solution.py:457
  83.2 0.0 collective-permute-done.14.got_1
  83.2 0.1 shard_map.165
  83.3 0.1 collective-permute-start.15
  83.4 0.0 copy-start
  83.4 0.0 copy-start.1
  83.4 0.0 copy-start.2
  83.4 1.6 %collective-permute-start.16 = (f32[832,128]{1,0:T(8,128)S(1)}, f32[832,128]{1,0:T(8,128)S(1)}, u32[]{:S(2)}, u32[]{:S(2)}) collective-permute-start(f32[832,128]{1,0:T(8,128)S(1)} %get-tuple-element.63.own_1), channel_id=1, source_target_pairs={{0,6},{1,49},{2,4},{3,51},{4,2},{5,53},{6,0},{7,55},{8,14},{9,57},... | collective-permute-start | bytes 1277960 | tf_op jit(solution)/shard_map/ppermute | solution.py:457
  85.0 5.3 %collective-permute-done.15.got_0 = f32[832,128]{1,0:T(8,128)S(1)} collective-permute-done((f32[832,128]{1,0:T(8,128)S(1)}, f32[832,128]{1,0:T(8,128)S(1)}, u32[]{:S(2)}, u32[]{:S(2)}) %collective-permute-start.15) | collective-permute-done | bytes 426016 | tf_op jit(solution)/shard_map/ppermute | solution.py:457
  90.4 1.3 %collective-permute-done.16.got_1 = f32[832,128]{1,0:T(8,128)S(1)} collective-permute-done((f32[832,128]{1,0:T(8,128)S(1)}, f32[832,128]{1,0:T(8,128)S(1)}, u32[]{:S(2)}, u32[]{:S(2)}) %collective-permute-start.16) | collective-permute-done | bytes 426016 | tf_op jit(solution)/shard_map/ppermute | solution.py:457
  91.7 0.2 shard_map.166.mine
  91.9 12.9 %collective-permute-start.17 = (f32[3328,128]{1,0:T(8,128)S(1)}, f32[3328,128]{1,0:T(8,128)S(1)}, u32[]{:S(2)}, u32[]{:S(2)}) collective-permute-start(f32[3328,128]{1,0:T(8,128)S(1)} %shard_map.166.mine), channel_id=1, source_target_pairs={{0,1},{1,0},{2,3},{3,2},{4,5},{5,4},{6,7},{7,6},{8,9},{9,8},{10,11... | collective-permute-start | bytes 5111816 | tf_op jit(solution)/shard_map/ppermute | solution.py:461
  104.8 3.2 %collective-permute-done.17.other = f32[3328,128]{1,0:T(8,128)S(1)} collective-permute-done((f32[3328,128]{1,0:T(8,128)S(1)}, f32[3328,128]{1,0:T(8,128)S(1)}, u32[]{:S(2)}, u32[]{:S(2)}) %collective-permute-start.17) | collective-permute-done | bytes 1703968 | tf_op jit(solution)/shard_map/ppermute | solution.py:461
  108.0 0.0 copy-done
  108.0 0.0 copy-done.1
  108.0 0.0 copy-done.2
  108.0 2.9 %shard_map.167 = (f32[4,256,256]{2,1,0:T(8,128)}, f32[512,1024]{1,0:T(8,128)}, f32[2,1024]{1,0:T(2,128)}) custom-call(f32[3328,128]{1,0:T(8,128)S(1)} %shard_map.166.mine, f32[3328,128]{1,0:T(8,128)S(1)} %collective-permute-done.17.other, f32[4,256,256]{2,1,0:T(8,128)S(1)} %copy-done.1, f32[512,1024]{1,0:T(8,128)S(1)} %copy-done, f32[2,1024]{1,0:T(2,128)S(1)} %copy-done.2), custom_call_target="tpu_custom_call" | custom-call | tf_op jit(solution)/shard_map/pallas_call | solution.py:281
  (6 shorter events, 0.2 us)
Async XLA Ops:
  7.9 6.5 %collective-permute-start = (f32[3328,128]{1,0:T(8,128)S(1)}, f32[3328,128]{1,0:T(8,128)S(1)}, u32[]{:S(2)}, u32[]{:S(2)}) collective-permute-start(f32[3328,128]{1,0:T(8,128)S(1)} %get-tuple-element.38), channel_id=1, source_target_pairs={{0,1},{1,0},{2,3},{3,2},{4,5},{5,4},{6,7},{7,6},{8,9},{9,8},{10,11... | collective-permute-start | bytes 5111816 | tf_op jit(solution)/shard_map/ppermute | solution.py:461
  14.6 7.4 %collective-permute-start.1 = (f32[832,128]{1,0:T(8,128)S(1)}, f32[832,128]{1,0:T(8,128)S(1)}, u32[]{:S(2)}, u32[]{:S(2)}) collective-permute-start(f32[832,128]{1,0:T(8,128)S(1)} %get-tuple-element.40), channel_id=1, source_target_pairs={{0,2},{1,17},{2,0},{3,19},{4,6},{5,21},{6,4},{7,23},{8,10},{9,25},... | collective-permute-start | bytes 1277960 | tf_op jit(solution)/shard_map/ppermute | solution.py:457
  14.7 8.6 %collective-permute-start.2 = (f32[832,128]{1,0:T(8,128)S(1)}, f32[832,128]{1,0:T(8,128)S(1)}, u32[]{:S(2)}, u32[]{:S(2)}) collective-permute-start(f32[832,128]{1,0:T(8,128)S(1)} %get-tuple-element.42), channel_id=1, source_target_pairs={{0,6},{1,49},{2,4},{3,51},{4,2},{5,53},{6,0},{7,55},{8,14},{9,57},... | collective-permute-start | bytes 1277960 | tf_op jit(solution)/shard_map/ppermute | solution.py:457
  23.2 33.1 %copy-start.3 = (f32[2,3080]{1,0:T(2,128)S(1)}, f32[2,3080]{1,0:T(2,128)}, u32[]{:S(2)}) copy-start(f32[2,3080]{1,0:T(2,128)} %moments.1) | copy-start | bytes 73924
  23.3 6.3 %collective-permute-start.3 = (f32[416,128]{1,0:T(8,128)S(1)}, f32[416,128]{1,0:T(8,128)S(1)}, u32[]{:S(2)}, u32[]{:S(2)}) collective-permute-start(f32[416,128]{1,0:T(8,128)S(1)} %get-tuple-element.44), channel_id=1, source_target_pairs={{0,6},{1,49},{2,4},{3,51},{4,2},{5,53},{6,0},{7,55},{8,14},{9,57},... | collective-permute-start | bytes 638984 | tf_op jit(solution)/shard_map/ppermute | solution.py:457
  24.8 5.0 %collective-permute-start.4 = (f32[416,128]{1,0:T(8,128)S(1)}, f32[416,128]{1,0:T(8,128)S(1)}, u32[]{:S(2)}, u32[]{:S(2)}) collective-permute-start(f32[416,128]{1,0:T(8,128)S(1)} %get-tuple-element.46), channel_id=1, source_target_pairs={{0,16},{1,3},{2,18},{3,1},{4,20},{5,7},{6,22},{7,5},{8,24},{9,11},... | collective-permute-start | bytes 638984 | tf_op jit(solution)/shard_map/ppermute | solution.py:457
  29.9 3.6 %collective-permute-start.5 = (f32[208,128]{1,0:T(8,128)S(1)}, f32[208,128]{1,0:T(8,128)S(1)}, u32[]{:S(2)}, u32[]{:S(2)}) collective-permute-start(f32[208,128]{1,0:T(8,128)S(1)} %get-tuple-element.48), channel_id=1, source_target_pairs={{0,16},{1,3},{2,18},{3,1},{4,20},{5,7},{6,22},{7,5},{8,24},{9,11},... | collective-permute-start | bytes 319496 | tf_op jit(solution)/shard_map/ppermute | solution.py:457
  30.9 4.8 %collective-permute-start.6 = (f32[208,128]{1,0:T(8,128)S(1)}, f32[208,128]{1,0:T(8,128)S(1)}, u32[]{:S(2)}, u32[]{:S(2)}) collective-permute-start(f32[208,128]{1,0:T(8,128)S(1)} %get-tuple-element.50), channel_id=1, source_target_pairs={{0,48},{1,7},{2,50},{3,5},{4,52},{5,3},{6,54},{7,1},{8,56},{9,15},... | collective-permute-start | bytes 319496 | tf_op jit(solution)/shard_map/ppermute | solution.py:457
  35.7 4.3 %collective-permute-start.7 = (f32[104,128]{1,0:T(8,128)S(1)}, f32[104,128]{1,0:T(8,128)S(1)}, u32[]{:S(2)}, u32[]{:S(2)}) collective-permute-start(f32[104,128]{1,0:T(8,128)S(1)} %get-tuple-element.52), channel_id=1, source_target_pairs={{0,48},{1,7},{2,50},{3,5},{4,52},{5,3},{6,54},{7,1},{8,56},{9,15},... | collective-permute-start | bytes 159752 | tf_op jit(solution)/shard_map/ppermute | solution.py:457
  37.6 3.0 %collective-permute-start.8 = (f32[104,128]{1,0:T(8,128)S(1)}, f32[104,128]{1,0:T(8,128)S(1)}, u32[]{:S(2)}, u32[]{:S(2)}) collective-permute-start(f32[104,128]{1,0:T(8,128)S(1)} %get-tuple-element.54), channel_id=1, source_target_pairs={{0,2},{1,17},{2,0},{3,19},{4,6},{5,21},{6,4},{7,23},{8,10},{9,25},... | collective-permute-start | bytes 159752 | tf_op jit(solution)/shard_map/ppermute | solution.py:457
  67.4 4.6 %collective-permute-start.9 = (f32[104,128]{1,0:T(8,128)S(1)}, f32[104,128]{1,0:T(8,128)S(1)}, u32[]{:S(2)}, u32[]{:S(2)}) collective-permute-start(f32[104,128]{1,0:T(8,128)S(1)} %get-tuple-element.56.own_0), channel_id=1, source_target_pairs={{0,48},{1,7},{2,50},{3,5},{4,52},{5,3},{6,54},{7,1},{8,56},{9,15},... | collective-permute-start | bytes 159752 | tf_op jit(solution)/shard_map/ppermute | solution.py:457
  68.7 3.3 %collective-permute-start.10 = (f32[104,128]{1,0:T(8,128)S(1)}, f32[104,128]{1,0:T(8,128)S(1)}, u32[]{:S(2)}, u32[]{:S(2)}) collective-permute-start(f32[104,128]{1,0:T(8,128)S(1)} %get-tuple-element.57.own_1), channel_id=1, source_target_pairs={{0,2},{1,17},{2,0},{3,19},{4,6},{5,21},{6,4},{7,23},{8,10},{9,25},... | collective-permute-start | bytes 159752 | tf_op jit(solution)/shard_map/ppermute | solution.py:457
  72.0 3.6 %collective-permute-start.11 = (f32[208,128]{1,0:T(8,128)S(1)}, f32[208,128]{1,0:T(8,128)S(1)}, u32[]{:S(2)}, u32[]{:S(2)}) collective-permute-start(f32[208,128]{1,0:T(8,128)S(1)} %get-tuple-element.58.own_0), channel_id=1, source_target_pairs={{0,16},{1,3},{2,18},{3,1},{4,20},{5,7},{6,22},{7,5},{8,24},{9,11},... | collective-permute-start | bytes 319496 | tf_op jit(solution)/shard_map/ppermute | solution.py:457
  72.1 5.0 %collective-permute-start.12 = (f32[208,128]{1,0:T(8,128)S(1)}, f32[208,128]{1,0:T(8,128)S(1)}, u32[]{:S(2)}, u32[]{:S(2)}) collective-permute-start(f32[208,128]{1,0:T(8,128)S(1)} %get-tuple-element.59.own_1), channel_id=1, source_target_pairs={{0,48},{1,7},{2,50},{3,5},{4,52},{5,3},{6,54},{7,1},{8,56},{9,15},... | collective-permute-start | bytes 319496 | tf_op jit(solution)/shard_map/ppermute | solution.py:457
  77.2 6.0 %collective-permute-start.13 = (f32[416,128]{1,0:T(8,128)S(1)}, f32[416,128]{1,0:T(8,128)S(1)}, u32[]{:S(2)}, u32[]{:S(2)}) collective-permute-start(f32[416,128]{1,0:T(8,128)S(1)} %get-tuple-element.60.own_0), channel_id=1, source_target_pairs={{0,6},{1,49},{2,4},{3,51},{4,2},{5,53},{6,0},{7,55},{8,14},{9,57},... | collective-permute-start | bytes 638984 | tf_op jit(solution)/shard_map/ppermute | solution.py:457
  78.5 4.7 %collective-permute-start.14 = (f32[416,128]{1,0:T(8,128)S(1)}, f32[416,128]{1,0:T(8,128)S(1)}, u32[]{:S(2)}, u32[]{:S(2)}) collective-permute-start(f32[416,128]{1,0:T(8,128)S(1)} %get-tuple-element.61.own_1), channel_id=1, source_target_pairs={{0,16},{1,3},{2,18},{3,1},{4,20},{5,7},{6,22},{7,5},{8,24},{9,11},... | collective-permute-start | bytes 638984 | tf_op jit(solution)/shard_map/ppermute | solution.py:457
  83.3 7.1 %collective-permute-start.15 = (f32[832,128]{1,0:T(8,128)S(1)}, f32[832,128]{1,0:T(8,128)S(1)}, u32[]{:S(2)}, u32[]{:S(2)}) collective-permute-start(f32[832,128]{1,0:T(8,128)S(1)} %get-tuple-element.62.own_0), channel_id=1, source_target_pairs={{0,2},{1,17},{2,0},{3,19},{4,6},{5,21},{6,4},{7,23},{8,10},{9,25},... | collective-permute-start | bytes 1277960 | tf_op jit(solution)/shard_map/ppermute | solution.py:457
  83.4 24.6 %copy-start = (f32[512,1024]{1,0:T(8,128)S(1)}, f32[512,1024]{1,0:T(8,128)}, u32[]{:S(2)}) copy-start(f32[512,1024]{1,0:T(8,128)} %dense.1) | copy-start | bytes 6291460
  83.4 24.6 %copy-start.1 = (f32[4,256,256]{2,1,0:T(8,128)S(1)}, f32[4,256,256]{2,1,0:T(8,128)}, u32[]{:S(2)}) copy-start(f32[4,256,256]{2,1,0:T(8,128)} %attn.1) | copy-start | bytes 3145732
  83.4 24.6 %copy-start.2 = (f32[2,1024]{1,0:T(2,128)S(1)}, f32[2,1024]{1,0:T(2,128)}, u32[]{:S(2)}) copy-start(f32[2,1024]{1,0:T(2,128)} %head.1) | copy-start | bytes 24580
  83.4 8.3 %collective-permute-start.16 = (f32[832,128]{1,0:T(8,128)S(1)}, f32[832,128]{1,0:T(8,128)S(1)}, u32[]{:S(2)}, u32[]{:S(2)}) collective-permute-start(f32[832,128]{1,0:T(8,128)S(1)} %get-tuple-element.63.own_1), channel_id=1, source_target_pairs={{0,6},{1,49},{2,4},{3,51},{4,2},{5,53},{6,0},{7,55},{8,14},{9,57},... | collective-permute-start | bytes 1277960 | tf_op jit(solution)/shard_map/ppermute | solution.py:457
  91.9 16.2 %collective-permute-start.17 = (f32[3328,128]{1,0:T(8,128)S(1)}, f32[3328,128]{1,0:T(8,128)S(1)}, u32[]{:S(2)}, u32[]{:S(2)}) collective-permute-start(f32[3328,128]{1,0:T(8,128)S(1)} %shard_map.166.mine), channel_id=1, source_target_pairs={{0,1},{1,0},{2,3},{3,2},{4,5},{5,4},{6,7},{7,6},{8,9},{9,8},{10,11... | collective-permute-start | bytes 5111816 | tf_op jit(solution)/shard_map/ppermute | solution.py:461
